TPU v7x, 128 devices: a whole 4x4x4 slice. The times are simulated.
128 devices in a mesh: shard: 32 (over z, x, core), replica: 4 (over y).
Axes of the slice: x: 4, y: 4, z: 4, core: 2. Of those that a mesh axis runs over, the one named last changes fastest.
Arguments:
- samples: bfloat16 [8192, 480, 128], P(('shard', 'replica')), may hold values from -6 to 6
- counts: int32 [8192], P(('shard', 'replica')), may hold values from 1 to 480
- buckets: int32 [8192, 480], P(('shard', 'replica')), may hold values from 0 to 127
- block_series: int32 [8192], P(('shard', 'replica')), may hold values from 0 to 255, as said below
- owner_map: int32 [256], replicated, may hold values from 0 to 255
Outputs:
- cold_stats: float32 [32, 4, 128, 4, 8, 128], P('shard', 'replica')
- sketches: float32 [256, 128, 128], P(('shard', 'replica'))
- live_rows: float32 [256], P(('shard', 'replica'))
Inputs may be any that keep to these rules, and one draw needn't show every extreme that they name: `block_series`: owner_map is a permutation of 0 to 255. With owner = owner_map[series] // 8, the 64 blocks of one device name at most 4 blocks of any one owner, and in every draw some owner gets exactly 4 blocks from every device.
All inputs are finite; a program needn't handle non-finite values.
Results may differ from a plain program's by a relative error of at most 0.0003.
Values may be sent and summed in bfloat16 or wider, within the bound.
A program may use at most 192 MiB of HBM per device.

v0:
```python
import jax
import jax.numpy as jnp
from jax import lax
from jax.sharding import PartitionSpec as P

BINS = 128


def copy_for_each(x, axis):
    copies = jnp.broadcast_to(x, (lax.axis_size(axis), *x.shape))
    return lax.all_to_all(copies, axis, split_axis=0, concat_axis=0, tiled=True)


def taken_together(x, axis):
    return copy_for_each(x, axis).sum(axis=0)


def packed_total(arrays, axis):
    flat, at, done = (jnp.concatenate([a.reshape(-1) for a in arrays]), 0, [])
    so_far = taken_together(flat, axis)
    for a in arrays:
        done.append(so_far[at : at + a.size].reshape(a.shape))
        at += a.size
    return tuple(done)


def minute_stats(values, counts):
    blocks, samples, lanes = values.shape
    minutes = samples // 60
    steps = jnp.arange(samples, dtype=jnp.int32)
    live = (steps[None, :] < counts[:, None]).reshape(blocks, minutes, 60, 1)
    data = values.astype(jnp.float32).reshape(blocks, minutes, 60, lanes)
    count = jnp.sum(jnp.where(live, jnp.float32(1.0), jnp.float32(0.0)), axis=2)
    count = jnp.broadcast_to(count, (blocks, minutes, lanes))
    total = jnp.sum(jnp.where(live, data, jnp.float32(0.0)), axis=2)
    lowest = jnp.min(jnp.where(live, data, jnp.inf), axis=2)
    highest = jnp.max(jnp.where(live, data, -jnp.inf), axis=2)
    filled = count > 0
    lowest = jnp.where(filled, lowest, jnp.float32(0.0))
    highest = jnp.where(filled, highest, jnp.float32(0.0))
    return jnp.stack([lowest, highest, total, count], axis=1)


def bucket_sketch(values, marks, counts):
    samples = values.shape[1]
    steps = lax.broadcasted_iota(jnp.int32, (1, 1, samples), 2)
    levels = lax.broadcasted_iota(jnp.int32, (1, BINS, 1), 1)
    table = ((marks[:, None, :] == levels) & (steps < counts[:, None, None])).astype(jnp.bfloat16)
    return jnp.einsum("nks,nsl->nkl", table, values, preferred_element_type=jnp.float32)


def body(samples, counts, buckets, block_series, owner_map):
    blocks = samples.shape[0]
    shards = lax.axis_size("shard")
    replicas = lax.axis_size("replica")
    cap = max(2, (2 * blocks + shards - 1) // shards)
    ser_own = owner_map.shape[0] // shards
    ser_dev = ser_own // replicas
    position = owner_map[block_series]
    owner = position // ser_own
    local = position % ser_own
    index = jnp.arange(blocks, dtype=jnp.int32)
    same = (owner[:, None] == owner[None, :]) & (index[None, :] < index[:, None])
    rank = jnp.sum(same.astype(jnp.int32), axis=1)
    slot = owner * cap + rank
    match = slot[:, None] == jnp.arange(shards * cap, dtype=jnp.int32)[None, :]
    source = jnp.sum(jnp.where(match, index[:, None], 0), axis=0)
    used = jnp.any(match, axis=0)
    series_levels = jnp.arange(ser_own, dtype=jnp.int32)
    stats_all = minute_stats(samples, counts)
    sketch_all = bucket_sketch(samples, buckets, counts)
    stats_buf = jnp.where(used[:, None, None, None], stats_all[source], 0.0)
    stats_buf = stats_buf.reshape((shards, cap) + stats_all.shape[1:])
    sketch_buf = jnp.where(used[:, None, None], sketch_all[source], 0.0)
    sketch_buf = sketch_buf.reshape((shards, cap) + sketch_all.shape[1:])
    place_buf = jnp.where(
        used[:, None], (local[source][:, None] == series_levels).astype(jnp.float32), 0.0
    )
    place_buf = place_buf.reshape(shards, cap, ser_own)
    rows_buf = jnp.where(used, counts[source], 0).astype(jnp.float32).reshape(shards, cap)
    stats, sketch, place, rows = (
        lax.all_to_all(stats_buf, "shard", split_axis=0, concat_axis=0, tiled=True),
        lax.all_to_all(sketch_buf, "shard", split_axis=0, concat_axis=0, tiled=True),
        lax.all_to_all(place_buf, "shard", split_axis=0, concat_axis=0, tiled=True),
        lax.all_to_all(rows_buf, "shard", split_axis=0, concat_axis=0, tiled=True),
    )
    series_sketch = jnp.einsum("sck,scbl->kbl", place, sketch, precision=lax.Precision.HIGHEST)
    series_rows = jnp.einsum("sck,sc->k", place, rows, precision=lax.Precision.HIGHEST)
    whole_sketch, whole_rows = packed_total((series_sketch, series_rows), "replica")
    start = lax.axis_index("replica") * ser_dev
    sketches = lax.dynamic_slice_in_dim(whole_sketch, start, ser_dev, 0)
    live_rows = lax.dynamic_slice_in_dim(whole_rows, start, ser_dev, 0)
    cold_stats = stats.reshape((1, 1, shards * cap) + stats.shape[2:])
    return (cold_stats, sketches, live_rows)


def solution(mesh):
    return jax.shard_map(
        body,
        mesh=mesh,
        in_specs=(
            P(("shard", "replica"), None, None),
            P(("shard", "replica")),
            P(("shard", "replica"), None),
            P(("shard", "replica")),
            P(),
        ),
        out_specs=(
            P("shard", "replica", None, None, None, None),
            P(("shard", "replica"), None, None),
            P(("shard", "replica")),
        ),
        check_vma=False,
    )
```

profile of v0, /device:TPU:0, one launch (start us, length us, event | category | flops | bytes accessed | tf_op | source)
XLA Modules:
  0.0 256.3 jit_solution(5117541132399780839)
XLA Ops:
  0.6 0.7 compare_select_fusion.1
  1.3 0.8 gather_fusion
  2.1 0.2 convert_reduce_fusion
  2.5 1.6 gather_fusion.4
  4.1 0.7 convert_element_type.26
  4.8 8.3 %all-to-all-start.3 = ((f32[32,1,4]{2,1,0:T(1,128)}), f32[32,1,4]{2,1,0:T(1,128)S(1)}, u32[]{:S(2)}, u32[]{:S(2)}) async-start(f32[32,1,4]{2,1,0:T(1,128)} %bitcast.14), calls=%async_computation.3 | async-start | bytes 32768 | tf_op jit(solution)/shard_map/all_to_all | solution.py:85
  13.2 0.7 iota_compare_fusion.1
  14.0 1.2 gather_fusion.2
  15.3 18.5 %fusion.4 = f32[64,128,128]{2,1,0:T(8,128)} fusion(bf16[64,480,128]{2,1,0:T(8,128)(2,1)} %param.5, s32[64,480]{1,0:T(8,128)} %param.7, pred[64,480]{1,0:T(8,128)(4,1)S(1)} %iota_compare_fusion.1), kind=kOutput, calls=%fused_computation.13 | convolution fusion | flops 1014497280 | bytes 12212224 | tf_op jit(solution)/shard_map/nks,nsl->nkl/dot_general | solution.py:49
  33.9 0.8 convert_select_fusion.3
  34.6 6.5 %gather_fusion.3 = f32[128,128,128]{2,1,0:T(8,128)} fusion(f32[64,128,128]{2,1,0:T(8,128)} %fusion.4, s32[1024]{0:T(1024)S(1)} %pad_clamp_fusion), kind=kCustom, calls=%fused_computation.3 | custom fusion | bytes 16777728 | tf_op jit(solution)/shard_map/gather | solution.py:74
  41.1 7.6 %all-to-all-start.1 = ((f32[32,4,8]{2,1,0:T(4,128)}), f32[32,4,8]{2,1,0:T(4,128)S(1)}, u32[]{:S(2)}, u32[]{:S(2)}) async-start(f32[32,4,8]{2,1,0:T(4,128)} %convert_select_fusion.3), calls=%async_computation.1 | async-start | bytes 131072 | tf_op jit(solution)/shard_map/all_to_all | solution.py:84
  48.7 14.8 %copy_select_fusion = f32[32,4,128,128]{3,1,2,0:T(4,128)} fusion(f32[32,4,128,128]{3,2,1,0:T(8,128)} %bitcast.35, pred[32,4]{1,0:T(8,128)(4,1)S(1)} %broadcast_in_dim.123), kind=kLoop, calls=%fused_computation.16 | loop fusion | flops 2097152 | bytes 16777344 | tf_op jit(solution)/shard_map/jit(_where)/select_n | solution.py:74
  63.5 7.6 %all-to-all-start.2 = ((f32[32,4,128,128]{3,1,2,0:T(4,128)}), f32[32,4,128,128]{3,1,2,0:T(4,128)}, u32[]{:S(2)}, u32[]{:S(2)}) async-start(f32[32,4,128,128]{3,1,2,0:T(4,128)} %copy_select_fusion), calls=%async_computation.2 | async-start | bytes 16777216 | tf_op jit(solution)/shard_map/all_to_all | solution.py:83
  71.0 9.3 %copy.53 = bf16[64,480,128]{2,0,1:T(8,128)(2,1)} copy(bf16[64,480,128]{2,1,0:T(8,128)(2,1)} %param.5) | data formatting | bytes 15728640 | tf_op args[0]
  81.0 8.5 %fusion = (f32[64,8,128]{2,0,1:T(8,128)S(1)}, f32[64,8,128]{2,0,1:T(8,128)S(1)}, f32[64,8,128]{2,0,1:T(8,128)S(1)}) fusion(bf16[64,8,60,128]{3,0,2,1:T(8,128)(2,1)} %bitcast.36, pred[64,8,60]{0,2,1:T(8,128)(4,1)S(1)} %broadcast_compare_fusion), kind=kLoop, calls=%fused_computation.8 | loop fusion | flops 27328512 | bytes 8681472 | tf_op jit(solution)/shard_map/reduce_min | solution.py:36
  89.5 0.2 copy.79
  89.6 0.4 bitcast_select_fusion.1
  90.2 0.8 gather_fusion.1
  91.0 1.5 broadcast_select_fusion
  92.7 0.1 convolution_bitcast_fusion
  92.9 83.8 %all-to-all-done.2 = f32[32,4,128,128]{3,1,2,0:T(4,128)} async-done(((f32[32,4,128,128]{3,1,2,0:T(4,128)}), f32[32,4,128,128]{3,1,2,0:T(4,128)}, u32[]{:S(2)}, u32[]{:S(2)}) %all-to-all-start.2) | async-done | bytes 8388640 | tf_op jit(solution)/shard_map/all_to_all | solution.py:83
  176.7 4.3 %all-to-all-start = ((f32[32,4,4,8,128]{4,3,2,1,0:T(8,128)}), f32[32,4,4,8,128]{4,3,2,1,0:T(8,128)S(1)}, u32[]{:S(2)}, u32[]{:S(2)}) async-start(f32[32,4,4,8,128]{4,3,2,1,0:T(8,128)} %broadcast_select_fusion), calls=%async_computation | async-start | bytes 4194304 | tf_op jit(solution)/shard_map/all_to_all | solution.py:82
  181.0 13.4 %fusion.10 = f32[8,128,128]{2,0,1:T(8,128)S(1)} fusion(f32[32,4,128,128]{3,1,2,0:T(4,128)} %all-to-all-done.2, f32[32,4,8]{0,2,1:T(8,128)S(1)} %copy.59), kind=kOutput, calls=%fused_computation.19 | convolution fusion | flops 201326592 | bytes 8916992 | tf_op jit(solution)/shard_map/sck,scbl->kbl/dot_general | solution.py:87
  194.6 16.2 %all-to-all-done = f32[32,4,4,8,128]{4,3,2,1,0:T(8,128)S(1)} async-done(((f32[32,4,4,8,128]{4,3,2,1,0:T(8,128)}), f32[32,4,4,8,128]{4,3,2,1,0:T(8,128)S(1)}, u32[]{:S(2)}, u32[]{:S(2)}) %all-to-all-start) | async-done | bytes 2097184 | tf_op jit(solution)/shard_map/all_to_all | solution.py:82
  210.8 3.5 %broadcast_in_dim.139 = f32[4,1,131080]{2,1,0:T(1,128)} broadcast(f32[131080]{0:T(1024)S(1)} %pad_maximum_fusion.1), dimensions={2} | broadcast | bytes 2621600 | tf_op jit(solution)/shard_map/broadcast_in_dim | solution.py:10
  214.3 4.5 %all-to-all-start.4 = ((f32[4,1,131080]{2,1,0:T(1,128)}), f32[4,1,131080]{2,1,0:T(1,128)S(1)}, u32[]{:S(2)}, u32[]{:S(2)}) async-start(f32[4,1,131080]{2,1,0:T(1,128)} %broadcast_in_dim.139), calls=%async_computation.4 | async-start | bytes 4198400 | tf_op jit(solution)/shard_map/all_to_all | solution.py:11
  218.8 24.8 %all-to-all-done.4 = f32[4,1,131080]{2,1,0:T(1,128)S(1)} async-done(((f32[4,1,131080]{2,1,0:T(1,128)}), f32[4,1,131080]{2,1,0:T(1,128)S(1)}, u32[]{:S(2)}, u32[]{:S(2)}) %all-to-all-start.4) | async-done | bytes 2097312 | tf_op jit(solution)/shard_map/all_to_all | solution.py:11
  243.6 8.4 %reduce_sum.52 = f32[131080]{0:T(1024)S(1)} reduce(f32[4,1,131080]{2,1,0:T(1,128)S(1)} %all-to-all-done.4, f32[]{:T(128)} %constant.50.clone.1), dimensions={0,1}, to_apply=%region_7.8 | reduce | flops 393240 | bytes 2621604 | tf_op jit(solution)/shard_map/reduce_sum | solution.py:15
  252.0 0.7 constant_dynamic-slice_fusion
  252.7 0.6 dynamic_slice.7
  253.3 3.1 %copy.81 = f32[1,1,128,4,8,128]{5,4,3,2,1,0:T(8,128)} copy(f32[1,1,128,4,8,128]{5,4,3,2,1,0:T(8,128)} %bitcast.38) | data formatting | bytes 4194304
  (33 shorter events, 1.5 us)
Async XLA Ops:
  0.6 0.7 copy-start
  4.8 36.3 %all-to-all-start.3 = ((f32[32,1,4]{2,1,0:T(1,128)}), f32[32,1,4]{2,1,0:T(1,128)S(1)}, u32[]{:S(2)}, u32[]{:S(2)}) async-start(f32[32,1,4]{2,1,0:T(1,128)} %bitcast.14), calls=%async_computation.3 | async-start | bytes 32768 | tf_op jit(solution)/shard_map/all_to_all | solution.py:85
  41.1 22.3 %all-to-all-start.1 = ((f32[32,4,8]{2,1,0:T(4,128)}), f32[32,4,8]{2,1,0:T(4,128)S(1)}, u32[]{:S(2)}, u32[]{:S(2)}) async-start(f32[32,4,8]{2,1,0:T(4,128)} %convert_select_fusion.3), calls=%async_computation.1 | async-start | bytes 131072 | tf_op jit(solution)/shard_map/all_to_all | solution.py:84
  63.5 113.2 %all-to-all-start.2 = ((f32[32,4,128,128]{3,1,2,0:T(4,128)}), f32[32,4,128,128]{3,1,2,0:T(4,128)}, u32[]{:S(2)}, u32[]{:S(2)}) async-start(f32[32,4,128,128]{3,1,2,0:T(4,128)} %copy_select_fusion), calls=%async_computation.2 | async-start | bytes 16777216 | tf_op jit(solution)/shard_map/all_to_all | solution.py:83
  71.0 9.4 %copy-start.1 = (s32[64]{0:T(128)S(1)}, s32[64]{0:T(128)}, u32[]{:S(2)}) copy-start(s32[64]{0:T(128)} %param.6) | copy-start | bytes 772
  176.7 34.1 %all-to-all-start = ((f32[32,4,4,8,128]{4,3,2,1,0:T(8,128)}), f32[32,4,4,8,128]{4,3,2,1,0:T(8,128)S(1)}, u32[]{:S(2)}, u32[]{:S(2)}) async-start(f32[32,4,4,8,128]{4,3,2,1,0:T(8,128)} %broadcast_select_fusion), calls=%async_computation | async-start | bytes 4194304 | tf_op jit(solution)/shard_map/all_to_all | solution.py:82
  210.8 3.5 %copy-start.2 = (f32[32,4,4,8,128]{4,3,2,1,0:T(8,128)}, f32[32,4,4,8,128]{4,3,2,1,0:T(8,128)S(1)}, u32[]{:S(2)}) copy-start(f32[32,4,4,8,128]{4,3,2,1,0:T(8,128)S(1)} %all-to-all-done) | copy-start | bytes 6291460
  214.3 29.3 %all-to-all-start.4 = ((f32[4,1,131080]{2,1,0:T(1,128)}), f32[4,1,131080]{2,1,0:T(1,128)S(1)}, u32[]{:S(2)}, u32[]{:S(2)}) async-start(f32[4,1,131080]{2,1,0:T(1,128)} %broadcast_in_dim.139), calls=%async_computation.4 | async-start | bytes 4198400 | tf_op jit(solution)/shard_map/all_to_all | solution.py:11
where the time goes:
time: 257 us; the launch traced here: 256 us
  waiting for transfers between devices  125 us (49%)
  other arithmetic  36.5 us (14%)
  starting transfers between devices  32.1 us (12%)
  matrix products  32.1 us (12%)
  local copies, waits for them, and re-layouts  29.8 us (12%)
    all_to_all x1, waiting for transfers between devices, body(): lax.all_to_all(sketch_buf, 'shard', split_axis=0, concat_axis=0, tiled=True)  83.8 us
    all_to_all x1, waiting for transfers between devices, copy_for_each(): return lax.all_to_all(copies, axis, split_axis=0, concat_axis=0, tiled=True)  24.8 us
    dot_general x1, matrix products, bucket_sketch(): jnp.einsum('nks,nsl->nkl', table, values, preferred_element_type=jnp.floa...  18.5 us
    all_to_all x1, waiting for transfers between devices, body(): lax.all_to_all(stats_buf, 'shard', split_axis=0, concat_axis=0, tiled=True)  16.2 us
    select_n x1, other arithmetic, body(): sketch_buf = jnp.where(used[:, None, None], sketch_all[source], 0.0)  14.8 us
    dot_general x1, matrix products, body(): jnp.einsum('sck,scbl->kbl', place, sketch, precision=lax.Precision.HIGHEST)  13.4 us
    unnamed x8, local copies, waits for them, and re-layouts  12.4 us
    reduce_min x1, other arithmetic, minute_stats(): lowest = jnp.min(jnp.where(live, data, jnp.inf), axis=2)  8.5 us
  transfers between devices with their start and end apart: 5, of which 3 were waited for; matrix products, arithmetic and copies ran while one was open for 30% of the time, Pallas kernels for 0%

commit v1 on v0

v1 whole, which is shorter than its diff:
```python
import functools

import jax
import jax.numpy as jnp
import numpy as np
from jax import lax
from jax.experimental import pallas as pl
from jax.experimental.pallas import tpu as pltpu
from jax.sharding import PartitionSpec as P

BINS = 128
LANES = 128
SAMPLES = 480
BLK = 64
SHARDS = 32
REPLICAS = 4
CAP = 4
DIMS = (("x", 0), ("z", 0), ("y", 0), ("x", 1), ("z", 1), ("y", 1))
ORDERS = tuple(tuple((p + s) % 6 for s in range(6)) for p in range(6))
ROWS = (16, 16, 32, 16, 16, 32)
STARTS = tuple(sum(ROWS[:p]) for p in range(6))
GRAY = {(0, 0): 0, (0, 1): 1, (1, 1): 2, (1, 0): 3}


def part_positions():
    table = np.zeros((6, 128), np.int32)
    for p, order in enumerate(ORDERS):
        for i in range(128):
            bits = {DIMS[d]: (i >> (6 - s)) & 1 for s, d in enumerate(order)}
            x, y, z = (GRAY[(bits[(a, 1)], bits[(a, 0)])] for a in "xyz")
            table[p, i] = (z * 4 + x) * 16 + y * 2 + (i & 1)
    return table


def local_kernel(idx_ref, samples_ref, marks_ref, table_ref, stats_ref, *, step):
    base = pl.program_id(0) * step
    rows = lax.broadcasted_iota(jnp.int32, (1, SAMPLES), 1)
    bins = lax.broadcasted_iota(jnp.int32, (BINS, SAMPLES), 0)
    first_row = lax.broadcasted_iota(jnp.int32, (16, SAMPLES), 0) * 60
    sub = lax.broadcasted_iota(jnp.int32, (8, LANES), 0)
    for j in range(step):
        b = base + j
        slot, fresh, place, count = idx_ref[0, b], idx_ref[1, b], idx_ref[2, b], idx_ref[3, b]
        x = samples_ref[j]
        live = rows < count
        marks = jnp.where(live, marks_ref[pl.ds(b, 1), :], -1)
        hot = jnp.where(bins == marks, 1.0, 0.0).astype(jnp.bfloat16)
        at = jnp.where(live, rows, -1)
        minute = jnp.where((at >= first_row) & (at < first_row + 60), 1.0, 0.0).astype(jnp.bfloat16)
        both = jnp.dot(jnp.concatenate([hot, minute], axis=0), x, preferred_element_type=jnp.float32)
        old = table_ref[slot]
        table_ref[slot] = jnp.where(fresh == 1, 0.0, old) + both[:BINS]
        total = both[BINS : BINS + 8]
        high = total.astype(jnp.bfloat16)
        low = (total - high.astype(jnp.float32)).astype(jnp.bfloat16)
        least = jnp.zeros((8, LANES), jnp.float32)
        most = jnp.zeros((8, LANES), jnp.float32)
        for q in range(4):
            lo = [None, None]
            hi = [None, None]
            for v in range(15):
                at_row = 120 * q + 8 * v
                val = x[at_row : at_row + 8].astype(jnp.float32)
                ok = sub < count - at_row
                small = jnp.where(ok, val, jnp.inf)
                large = jnp.where(ok, val, -jnp.inf)
                for h in (0, 1):
                    if (h == 0 and v > 7) or (h == 1 and v < 7):
                        continue
                    s, g = small, large
                    if v == 7:
                        mine = (sub < 4) if h == 0 else (sub >= 4)
                        s, g = jnp.where(mine, s, jnp.inf), jnp.where(mine, g, -jnp.inf)
                    lo[h] = s if lo[h] is None else jnp.minimum(lo[h], s)
                    hi[h] = g if hi[h] is None else jnp.maximum(hi[h], g)
            for h in (0, 1):
                m = 2 * q + h
                least = jnp.where(sub == m, jnp.min(lo[h], axis=0, keepdims=True), least)
                most = jnp.where(sub == m, jnp.max(hi[h], axis=0, keepdims=True), most)
        stats_ref[place] = jnp.concatenate(
            [least.astype(jnp.bfloat16), most.astype(jnp.bfloat16), high, low], axis=0
        )


def local_call(idx, samples, marks):
    step = 4
    return pl.pallas_call(
        functools.partial(local_kernel, step=step),
        grid=(BLK // step,),
        in_specs=[
            pl.BlockSpec(memory_space=pltpu.SMEM),
            pl.BlockSpec((step, SAMPLES, LANES), lambda i: (i, 0, 0)),
            pl.BlockSpec((BLK, SAMPLES), lambda i: (0, 0)),
        ],
        out_specs=[
            pl.BlockSpec((SHARDS * CAP, BINS, LANES), lambda i: (0, 0, 0)),
            pl.BlockSpec((SHARDS * CAP, 32, LANES), lambda i: (0, 0, 0)),
        ],
        out_shape=[
            jax.ShapeDtypeStruct((SHARDS * CAP, BINS, LANES), jnp.float32),
            jax.ShapeDtypeStruct((SHARDS * CAP, 32, LANES), jnp.bfloat16),
        ],
        compiler_params=pltpu.CompilerParams(vmem_limit_bytes=56 * 2**20),
        name="local_stats",
    )(idx, samples, marks)


def exchange_kernel(
    own_idx, prt_idx, table, stats, meta, live,
    sk_out, stats_out, meta_out, live_out,
    *scratch,
):
    own, prt, acc, got = scratch[0:6], scratch[6:12], scratch[12:18], scratch[18:24]
    mine_st, mine_meta, rows_in, lbuf, lgot = scratch[24:29]
    own_sem, d2d_send, d2d_recv, cube_send, cube_recv, st_send, st_recv, l_send, l_recv, loc_sem = scratch[29:39]
    shard = lax.axis_index("shard")
    y = lax.axis_index("replica")
    core = lax.rem(shard, 2)
    x = lax.rem(lax.div(shard, 2), 4)
    z = lax.div(shard, 8)
    where_at = {"x": x, "y": y, "z": z}

    def other(dim):
        axis, bit = dim
        v = where_at[axis]
        high = lax.div(v, 2)
        if bit == 0:
            mine = lax.rem(v + high, 2)
            w = v + 1 - 2 * lax.rem(v, 2)
        else:
            mine = high
            w = 3 - v
        if axis == "x":
            return {"shard": shard + (w - v) * 2, "replica": y}, mine
        if axis == "z":
            return {"shard": shard + (w - v) * 8, "replica": y}, mine
        return {"shard": shard, "replica": w}, mine

    across = [other(d) for d in DIMS]
    partner = {"shard": shard + 1 - 2 * core, "replica": y}

    barrier = pltpu.get_barrier_semaphore()

    def greet(d, _):
        pl.semaphore_signal(barrier, inc=1, device_id={"shard": lax.rem(shard + d, SHARDS), "replica": y})
        return 0

    lax.fori_loop(1, SHARDS, greet, 0)
    for d in (2, 5):
        pl.semaphore_signal(barrier, inc=1, device_id=across[d][0])
    own_copies = []
    for p in range(6):
        rows = pl.ds(STARTS[p], ROWS[p])
        c = pltpu.make_async_copy(table.at[core, :, rows], own[p].at[pl.ds(0, BLK)], own_sem.at[p])
        c.start()
        own_copies.append(c)
    st_in = pltpu.make_async_copy(stats.at[shard], mine_st, loc_sem.at[0])
    st_in.start()
    meta_in = pltpu.make_async_copy(meta.at[shard], mine_meta, loc_sem.at[1])
    meta_in.start()
    live_in = pltpu.make_async_copy(live, rows_in, loc_sem.at[2])
    live_in.start()
    for p in range(6):
        own[p][BLK] = jnp.zeros((ROWS[p], LANES), jnp.float32)
        prt[p][BLK] = jnp.zeros((ROWS[p], LANES), jnp.float32)
    pl.semaphore_wait(barrier, SHARDS + 1)

    def d2d(p):
        rows = pl.ds(STARTS[p], ROWS[p])
        return pltpu.make_async_remote_copy(
            table.at[1 - core, :, rows], prt[p].at[pl.ds(0, BLK)], d2d_send.at[p], d2d_recv.at[p], device_id=partner,
        )

    parts = (2, 5, 0, 1, 3, 4)
    d2d_copies = {p: d2d(p) for p in parts}
    for p in parts:
        d2d_copies[p].start()

    def st_copy(d, dst_shard, src_slot):
        return pltpu.make_async_remote_copy(
            stats.at[dst_shard], stats_out.at[src_slot], st_send.at[0, d], st_recv.at[0, d],
            device_id={"shard": dst_shard, "replica": y},
        )

    def meta_copy(d, dst_shard, src_slot):
        return pltpu.make_async_remote_copy(
            meta.at[dst_shard], meta_out.at[src_slot], st_send.at[1, d], st_recv.at[1, d],
            device_id={"shard": dst_shard, "replica": y},
        )

    def send_stats(d, _):
        to = lax.rem(shard + d, SHARDS)
        st_copy(d, to, shard).start()
        meta_copy(d, to, shard).start()
        return 0

    lax.fori_loop(1, SHARDS, send_stats, 0)
    st_in.wait()
    st_back = pltpu.make_async_copy(mine_st, stats_out.at[shard], loc_sem.at[3])
    st_back.start()
    meta_in.wait()
    meta_back = pltpu.make_async_copy(mine_meta, meta_out.at[shard], loc_sem.at[4])
    meta_back.start()
    live_in.wait()

    def live_copy(s, src, device):
        return pltpu.make_async_remote_copy(src, lgot.at[s], l_send.at[s], l_recv.at[s], device_id=device)

    live_copies = [live_copy(0, rows_in.at[1 - core], partner)]
    live_copies[0].start()

    bases = [[None] * 7 for _ in range(6)]
    copies = [[None] * 6 for _ in range(6)]

    def densify(p, lo):
        def body(i, _):
            for u in range(8):
                e = lo + i * 8 + u
                acc[p][e] = own[p][own_idx[p * 128 + e]] + prt[p][prt_idx[p * 128 + e]]
            return 0

        lax.fori_loop(0, 8, body, 0)

    def add_in(p, at, lo, n):
        unroll = min(n, 8)

        def body(i, _):
            for u in range(unroll):
                e = i * unroll + u
                acc[p][at + e] = acc[p][at + e] + got[p][lo + e]
            return 0

        lax.fori_loop(0, n // unroll, body, 0)

    def send(p, s):
        device, bit = across[ORDERS[p][s]]
        half = 64 >> s
        base = bases[p][s]
        c = pltpu.make_async_remote_copy(
            acc[p].at[pl.ds(base + (1 - bit) * half, half)],
            got[p].at[pl.ds(128 - (128 >> s), half)],
            cube_send.at[p, s], cube_recv.at[p, s], device_id=device,
        )
        c.start()
        copies[p][s] = c
        bases[p][s + 1] = base + bit * half

    for p in parts:
        own_copies[p].wait()
        d2d_copies[p].wait_recv()
        bases[p][0] = 0
        bit = across[ORDERS[p][0]][1]
        densify(p, (1 - bit) * 64)
        send(p, 0)
        densify(p, bit * 64)

    live_copies[0].wait_recv()
    lbuf[0] = rows_in[core] + lgot[0]
    for s in range(1, 7):
        live_copies.append(live_copy(s, lbuf.at[s - 1], across[ORDERS[0][s - 1]][0]))
        live_copies[s].start()
        for p in parts:
            copies[p][s - 1].wait_recv()
            half = 64 >> (s - 1)
            lo = 128 - (128 >> (s - 1))
            base = bases[p][s]
            if s < 6:
                quarter = half // 2
                bit = across[ORDERS[p][s]][1]
                add_in(p, base + (1 - bit) * quarter, lo + (1 - bit) * quarter, quarter)
                send(p, s)
                add_in(p, base + bit * quarter, lo + bit * quarter, quarter)
            else:
                for k in range(2):
                    sk_out[k, STARTS[p] : STARTS[p] + ROWS[p], :] = acc[p][base + k] + got[p][lo + k]
        live_copies[s].wait_recv()
        lbuf[s] = lbuf[s - 1] + lgot[s]
    live_out[...] = lbuf[6]

    def wait_stats(d, _):
        came = lax.rem(shard - d + SHARDS, SHARDS)
        st_copy(d, shard, came).wait_recv()
        meta_copy(d, shard, came).wait_recv()
        return 0

    lax.fori_loop(1, SHARDS, wait_stats, 0)

    def wait_sends(d, _):
        to = lax.rem(shard + d, SHARDS)
        st_copy(d, to, shard).wait_send()
        meta_copy(d, to, shard).wait_send()
        return 0

    lax.fori_loop(1, SHARDS, wait_sends, 0)
    st_back.wait()
    meta_back.wait()
    for c in live_copies:
        c.wait_send()
    for p in range(6):
        d2d_copies[p].wait_send()
        for s in range(6):
            copies[p][s].wait_send()


def exchange_call(own_idx, prt_idx, table, stats, meta, live):
    any_ = pl.BlockSpec(memory_space=pl.ANY)
    vmem = pl.BlockSpec(memory_space=pltpu.VMEM)
    smem = pl.BlockSpec(memory_space=pltpu.SMEM)
    f32 = jnp.float32
    scratch = (
        [pltpu.VMEM((BLK + 1, r, LANES), f32) for r in ROWS]
        + [pltpu.VMEM((BLK + 1, r, LANES), f32) for r in ROWS]
        + [pltpu.VMEM((128, r, LANES), f32) for r in ROWS]
        + [pltpu.VMEM((126, r, LANES), f32) for r in ROWS]
        + [
            pltpu.VMEM((CAP, 32, LANES), jnp.bfloat16),
            pltpu.VMEM((1, LANES), f32),
            pltpu.VMEM((2, 1, LANES), f32),
            pltpu.VMEM((7, 1, LANES), f32),
            pltpu.VMEM((7, 1, LANES), f32),
        ]
        + [
            pltpu.SemaphoreType.DMA((6,)),
            pltpu.SemaphoreType.DMA((6,)),
            pltpu.SemaphoreType.DMA((6,)),
            pltpu.SemaphoreType.DMA((6, 6)),
            pltpu.SemaphoreType.DMA((6, 6)),
            pltpu.SemaphoreType.DMA((2, SHARDS)),
            pltpu.SemaphoreType.DMA((2, SHARDS)),
            pltpu.SemaphoreType.DMA((7,)),
            pltpu.SemaphoreType.DMA((7,)),
            pltpu.SemaphoreType.DMA((5,)),
        ]
    )
    return pl.pallas_call(
        exchange_kernel,
        in_specs=[smem, smem, any_, any_, any_, any_],
        out_specs=[vmem, any_, any_, vmem],
        out_shape=[
            jax.ShapeDtypeStruct((2, BINS, LANES), f32),
            jax.ShapeDtypeStruct((SHARDS, CAP, 32, LANES), jnp.bfloat16),
            jax.ShapeDtypeStruct((SHARDS, 1, LANES), f32),
            jax.ShapeDtypeStruct((1, LANES), f32),
        ],
        scratch_shapes=scratch,
        compiler_params=pltpu.CompilerParams(
            collective_id=0, has_side_effects=True, vmem_limit_bytes=56 * 2**20
        ),
        name="exchange",
    )(own_idx, prt_idx, table, stats, meta, live)


def finish_kernel(counts, stats_ref, sk_ref, live_ref, cold_ref, sk_out, live_out, *, step):
    i = pl.program_id(0)
    minute = lax.broadcasted_iota(jnp.int32, (8, LANES), 0).astype(jnp.float32) * 60.0
    for j in range(step):
        at = i * step + j
        n = counts[lax.div(at, CAP), 0, lax.rem(at, CAP)]
        count = jnp.clip(n - minute, 0.0, 60.0)
        filled = count > 0
        st = stats_ref[j].astype(jnp.float32)
        cold_ref[j, 0] = jnp.where(filled, st[0:8], 0.0)
        cold_ref[j, 1] = jnp.where(filled, st[8:16], 0.0)
        cold_ref[j, 2] = jnp.where(filled, st[16:24] + st[24:32], 0.0)
        cold_ref[j, 3] = count

    @pl.when(i == 0)
    def _():
        sk_out[...] = sk_ref[...]
        at = lax.div(lax.axis_index("shard"), 2) * 8 + lax.axis_index("replica") * 2
        lane = lax.broadcasted_iota(jnp.int32, (1, LANES), 1)
        for k in range(2):
            live_out[k] = jnp.sum(jnp.where(lane == at + k, live_ref[...], 0.0))


def finish_call(counts, stats, sketches, live):
    step = 16
    return pl.pallas_call(
        functools.partial(finish_kernel, step=step),
        grid=(SHARDS * CAP // step,),
        in_specs=[
            pl.BlockSpec(memory_space=pltpu.SMEM),
            pl.BlockSpec((step, 32, LANES), lambda i: (i, 0, 0)),
            pl.BlockSpec((2, BINS, LANES), lambda i: (0, 0, 0)),
            pl.BlockSpec((1, LANES), lambda i: (0, 0)),
        ],
        out_specs=[
            pl.BlockSpec((step, 4, 8, LANES), lambda i: (i, 0, 0, 0)),
            pl.BlockSpec((2, BINS, LANES), lambda i: (0, 0, 0)),
            pl.BlockSpec(memory_space=pltpu.SMEM),
        ],
        out_shape=[
            jax.ShapeDtypeStruct((SHARDS * CAP, 4, 8, LANES), jnp.float32),
            jax.ShapeDtypeStruct((2, BINS, LANES), jnp.float32),
            jax.ShapeDtypeStruct((2,), jnp.float32),
        ],
        name="finish",
    )(counts, stats, sketches, live)


def positions_of(block_series, owner_map):
    series = jnp.arange(owner_map.shape[0], dtype=jnp.int32)
    return jnp.sum(jnp.where(block_series[:, None] == series[None, :], owner_map[None, :], 0), axis=1)


def slots_of(position):
    owner = position // 8
    index = jnp.arange(BLK, dtype=jnp.int32)
    earlier = index[None, :] < index[:, None]
    rank = jnp.sum(((owner[:, None] == owner[None, :]) & earlier).astype(jnp.int32), axis=1)
    return owner, rank, (owner // 2) * CAP + rank


def body(samples, counts, buckets, block_series, owner_map):
    core = lax.axis_index("shard") % 2
    swap = [(i, i ^ 1) for i in range(SHARDS)]
    their_series = lax.ppermute(block_series, "shard", swap)
    position = positions_of(block_series, owner_map)
    owner, rank, half_slot = slots_of(position)
    same = position[:, None] == position[None, :]
    first_slot = jnp.min(jnp.where(same, half_slot[None, :], 2 * BLK), axis=1)
    fresh = (first_slot == half_slot).astype(jnp.int32)
    place = owner * CAP + rank
    idx = jnp.stack([(owner % 2) * BLK + first_slot, fresh, place, counts])
    table, stats = local_call(idx, samples, buckets)

    target = jnp.asarray(part_positions().reshape(-1)) + core * 8

    def entries(pos, slot):
        hit = target[:, None] == pos[None, :]
        return jnp.min(jnp.where(hit, slot[None, :], BLK), axis=1)

    own_idx = entries(position, half_slot)
    their_position = positions_of(their_series, owner_map)
    prt_idx = entries(their_position, slots_of(their_position)[2])
    rows = counts.astype(jnp.float32)
    lane = np.arange(128)
    live_at = jnp.asarray(np.stack([(lane // 8) * 16 + r * 8 + lane % 8 for r in (0, 1)]).astype(np.int32))
    live = jnp.sum(jnp.where(live_at[:, :, None] == position[None, None, :], rows[None, None, :], 0.0), axis=2)
    at = np.where(lane[None, :] < CAP, np.arange(SHARDS)[:, None] * CAP + lane[None, :], -1).astype(np.int32)
    meta = jnp.sum(jnp.where(jnp.asarray(at)[:, :, None] == place[None, None, :], rows[None, None, :], 0.0), axis=2)
    sk, st, got_counts, got_live = exchange_call(
        own_idx, prt_idx,
        table.reshape(2, BLK, BINS, LANES), stats.reshape(SHARDS, CAP, 32, LANES),
        meta.reshape(SHARDS, 1, LANES), live.reshape(2, 1, LANES),
    )
    cold, sketches, live_rows = finish_call(got_counts, st.reshape(SHARDS * CAP, 32, LANES), sk, got_live)
    return cold.reshape(1, 1, SHARDS * CAP, 4, 8, LANES), sketches, live_rows


def solution(mesh):
    return jax.shard_map(
        body,
        mesh=mesh,
        in_specs=(
            P(("shard", "replica"), None, None),
            P(("shard", "replica")),
            P(("shard", "replica"), None),
            P(("shard", "replica")),
            P(),
        ),
        out_specs=(
            P("shard", "replica", None, None, None, None),
            P(("shard", "replica"), None, None),
            P(("shard", "replica")),
        ),
        check_vma=False,
    )
```

time: 257 us -> 105 us (0.41)
  waiting for transfers between devices: 125 us -> 0.01 us
  Pallas kernels: 0 us -> 95.9 us
  matrix products: 32.1 us -> 0 us
  starting transfers between devices: 32.1 us -> 0.09 us
  local copies, waits for them, and re-layouts: 29.8 us -> 0 us
  other arithmetic: 36.5 us -> 7.62 us
    all_to_all x5 -> x0, waiting for transfers between devices: 125 us -> none  [the longest x1 83.8 us: body(): lax.all_to_all(sketch_buf, 'shard', split_axis=0, concat_axis=0, tiled=True)]
    pallas_call x0 -> x3, Pallas kernels: none -> 95.9 us  [the longest x1 72.4 us: exchange_call(): pl.pallas_call(exchange_kernel, in_specs=[smem, smem, any_, any_, any_, a...]
    all_to_all x5 -> x0, starting transfers between devices: 32.1 us -> none  [the longest x1 8.28 us: body(): lax.all_to_all(rows_buf, 'shard', split_axis=0, concat_axis=0, tiled=True)]
    dot_general x3 -> x0, matrix products: 32.1 us -> none  [the longest x1 18.5 us: bucket_sketch(): jnp.einsum('nks,nsl->nkl', table, values, preferred_element_type=jnp.floa...]
    select_n x7 -> x1, other arithmetic: 18.1 us -> 0.01 us  [slots_of(): owner = position // 8]
    unnamed x8 -> x0, local copies, waits for them, and re-layouts: 12.4 us -> none
    gather x5 -> x0, local copies, waits for them, and re-layouts: 10.9 us -> none  [the longest x1 6.48 us: body(): sketch_buf = jnp.where(used[:, None, None], sketch_all[source], 0.0)]
    reduce_min x1 -> x2, other arithmetic: 8.5 us -> 0.91 us  [the longest x1 0.73 us: entries(): return jnp.min(jnp.where(hit, slot[None, :], BLK), axis=1)]
  transfers between devices with their start and end apart: 5 -> 1, of which waited for: 3 -> 0; matrix products, arithmetic and copies ran while one was open for 30% -> 1% of each run, Pallas kernels for 0% -> 0%
where the time goes in v1:
time: 105 us; the launch traced here: 104 us
  Pallas kernels  95.9 us (91%)
  other arithmetic  7.62 us (7%)
    pallas_call x1, Pallas kernels, exchange_call(): pl.pallas_call(exchange_kernel, in_specs=[smem, smem, any_, any_, any_, a...  72.4 us
    pallas_call x1, Pallas kernels, local_call(): pl.pallas_call(functools.partial(local_kernel, step=step), grid=(BLK // s...  17.3 us
    pallas_call x1, Pallas kernels, finish_call(): pl.pallas_call(functools.partial(finish_kernel, step=step), grid=(SHARDS...  6.1 us
  transfers between devices with their start and end apart: 1, of which 0 were waited for; matrix products, arithmetic and copies ran while one was open for 1% of the time, Pallas kernels for 0%

profile of v1, /device:TPU:0, one launch (start us, length us, event | category | flops | bytes accessed | tf_op | source)
XLA Modules:
  0.0 104.3 jit_solution(3992284113627363401)
XLA Ops:
  0.6 0.1 collective-permute-start
  0.7 0.7 broadcast_add_fusion
  1.4 0.7 convert_element_type.22
  2.1 0.0 collective-permute-done
  2.1 0.9 select_reduce_fusion.4
  3.0 0.2 convert_reduce_fusion.1
  3.2 0.2 select_reduce_fusion.6
  3.4 0.2 convert_reduce_fusion
  3.6 1.3 %select_reduce_fusion.3 = f32[2,128]{1,0:T(2,128)} fusion(f32[64]{0:T(128)S(1)} %convert_element_type.22, s32[2,128]{1,0:T(2,128)} %constant.83.clone, s32[64]{0:T(128)S(1)} %get-tuple-element.24), kind=kLoop, calls=%fused_computation.3 | loop fusion | flops 48896 | bytes 2560 | tf_op jit(solution)/shard_map/reduce_sum | solution.py:439
  4.9 0.7 select_reduce_fusion.1
  5.7 1.5 %select_reduce_fusion = f32[32,128]{1,0:T(8,128)} fusion(f32[64]{0:T(128)S(1)} %convert_element_type.22, s32[32,128]{1,0:T(8,128)} %constant.84.clone, s32[64]{0:T(128)S(1)} %get-tuple-element.25), kind=kLoop, calls=%fused_computation | loop fusion | flops 782336 | bytes 33280 | tf_op jit(solution)/shard_map/reduce_sum | solution.py:441
  7.2 1.2 %pad_add_fusion.idx_ref = s32[4,64]{1,0:T(4,128)} fusion(s32[1,64]{1,0:T(1,128)} %bitcast.38, s32[1,64]{1,0:T(1,128)S(1)} %get-tuple-element.28, s32[1,64]{1,0:T(1,128)S(1)} %compare_convert_fusion, s32[1,64]{1,0:T(1,128)S(1)} %get-tuple-element.27), kind=kLoop, calls=%fused_computation.14 | loop fusion | flops 768 | bytes 2048 | tf_op jit(solution)/shard_map/stack | solution.py:424
  8.4 17.3 %local_stats.1 = (f32[128,128,128]{2,1,0:T(8,128)}, bf16[128,32,128]{2,1,0:T(8,128)(2,1)}) custom-call(s32[4,64]{1,0:T(4,128)} %pad_add_fusion.idx_ref, bf16[64,480,128]{2,1,0:T(8,128)(2,1)} %samples_ref.1, s32[64,480]{1,0:T(8,128)} %marks_ref.1), custom_call_target="tpu_custom_call" | custom-call | tf_op jit(solution)/shard_map/local_stats/pallas_call | solution.py:87
  25.8 72.4 %exchange.1 = (f32[2,128,128]{2,1,0:T(8,128)}, bf16[32,4,32,128]{3,2,1,0:T(8,128)(2,1)}, f32[32,1,128]{2,1,0:T(1,128)}, f32[1,128]{1,0:T(1,128)}) custom-call(s32[768]{0:T(1024)} %get-tuple-element.22.own_idx, s32[768]{0:T(1024)} %get-tuple-element.21.prt_idx, f32[2,64,128,128]{3,2,1,0:T(8,128)} %bitcast.33, bf16[32,4,32,128]{3,2,1,0:T(8,128)(2,1)} %bitcast.35, ...), custom_call_target="tpu_custom_call" | custom-call | tf_op jit(solution)/shard_map/exchange/pallas_call | solution.py:335
  98.2 6.1 %finish.1 = (f32[128,4,8,128]{3,2,1,0:T(8,128)}, f32[2,128,128]{2,1,0:T(8,128)}, f32[2]{0:T(128)}) custom-call(f32[32,1,128]{2,1,0:T(1,128)} %get-tuple-element.14.counts, bf16[128,32,128]{2,1,0:T(8,128)(2,1)} %bitcast.34, f32[2,128,128]{2,1,0:T(8,128)} %get-tuple-element.16.sk_ref, f32[1,128]{1,0:T(1,128)} %get-tuple-element.17.live_ref), custom_call_target="tpu_custom_call" | custom-call | tf_op jit(solution)/shard_map/finish/pallas_call | solution.py:378
  (5 shorter events, 0.1 us)
Async XLA Ops:
  0.6 1.5 %collective-permute-start = (s32[64]{0:T(128)}, s32[64]{0:T(128)S(1)}, u32[]{:S(2)}, u32[]{:S(2)}) collective-permute-start(s32[64]{0:T(128)} %param.11), channel_id=1, source_target_pairs={{0,4},{4,0},{8,12},{12,8},{16,20},{20,16},{24,28},{28,24},{32,36},... | collective-permute-start | bytes 776 | tf_op jit(solution)/shard_map/ppermute | solution.py:417

commit v2 on v1

--- a/solution.py
+++ b/solution.py
@@ -16,14 +16,19 @@
 REPLICAS = 4
 CAP = 4
 DIMS = (("x", 0), ("z", 0), ("y", 0), ("x", 1), ("z", 1), ("y", 1))
-ORDERS = tuple(tuple((p + s) % 6 for s in range(6)) for p in range(6))
-ROWS = (16, 16, 32, 16, 16, 32)
-STARTS = tuple(sum(ROWS[:p]) for p in range(6))
+ORDERS = (
+    (5, 2, 4, 0, 3, 1), (5, 4, 1, 2, 0, 3), (2, 5, 1, 3, 4, 0), (0, 1, 4, 3, 5, 2),
+    (2, 0, 3, 4, 1, 5), (3, 2, 5, 4, 1, 0), (4, 3, 0, 5, 2, 1), (1, 5, 2, 0, 3, 4),
+)
+PARTS = len(ORDERS)
+ROWS = BINS // PARTS
+LEVELS = 32766.0
+TINY = 1e-33
 GRAY = {(0, 0): 0, (0, 1): 1, (1, 1): 2, (1, 0): 3}
 
 
 def part_positions():
-    table = np.zeros((6, 128), np.int32)
+    table = np.zeros((PARTS, 128), np.int32)
     for p, order in enumerate(ORDERS):
         for i in range(128):
             bits = {DIMS[d]: (i >> (6 - s)) & 1 for s, d in enumerate(order)}
@@ -110,9 +115,9 @@
     sk_out, stats_out, meta_out, live_out,
     *scratch,
 ):
-    own, prt, acc, got = scratch[0:6], scratch[6:12], scratch[12:18], scratch[18:24]
-    mine_st, mine_meta, rows_in, lbuf, lgot = scratch[24:29]
-    own_sem, d2d_send, d2d_recv, cube_send, cube_recv, st_send, st_recv, l_send, l_recv, loc_sem = scratch[29:39]
+    own, prt, acc, out, outs, got, gots = (scratch[PARTS * i : PARTS * (i + 1)] for i in range(7))
+    mine_st, mine_meta, rows_in, lbuf, lgot = scratch[7 * PARTS : 7 * PARTS + 5]
+    (own_sem, d2d_send, d2d_recv, cube_send, cube_recv, st_send, st_recv, l_send, l_recv, loc_sem) = scratch[7 * PARTS + 5 :]
     shard = lax.axis_index("shard")
     y = lax.axis_index("replica")
     core = lax.rem(shard, 2)
@@ -149,8 +154,8 @@
     for d in (2, 5):
         pl.semaphore_signal(barrier, inc=1, device_id=across[d][0])
     own_copies = []
-    for p in range(6):
-        rows = pl.ds(STARTS[p], ROWS[p])
+    for p in range(PARTS):
+        rows = pl.ds(p * ROWS, ROWS)
         c = pltpu.make_async_copy(table.at[core, :, rows], own[p].at[pl.ds(0, BLK)], own_sem.at[p])
         c.start()
         own_copies.append(c)
@@ -160,18 +165,18 @@
     meta_in.start()
     live_in = pltpu.make_async_copy(live, rows_in, loc_sem.at[2])
     live_in.start()
-    for p in range(6):
-        own[p][BLK] = jnp.zeros((ROWS[p], LANES), jnp.float32)
-        prt[p][BLK] = jnp.zeros((ROWS[p], LANES), jnp.float32)
+    for p in range(PARTS):
+        own[p][BLK] = jnp.zeros((ROWS, LANES), jnp.float32)
+        prt[p][BLK] = jnp.zeros((ROWS, LANES), jnp.float32)
     pl.semaphore_wait(barrier, SHARDS + 1)
 
     def d2d(p):
-        rows = pl.ds(STARTS[p], ROWS[p])
+        rows = pl.ds(p * ROWS, ROWS)
         return pltpu.make_async_remote_copy(
             table.at[1 - core, :, rows], prt[p].at[pl.ds(0, BLK)], d2d_send.at[p], d2d_recv.at[p], device_id=partner,
         )
 
-    parts = (2, 5, 0, 1, 3, 4)
+    parts = tuple(range(PARTS))
     d2d_copies = {p: d2d(p) for p in parts}
     for p in parts:
         d2d_copies[p].start()
@@ -209,48 +214,75 @@
     live_copies = [live_copy(0, rows_in.at[1 - core], partner)]
     live_copies[0].start()
 
-    bases = [[None] * 7 for _ in range(6)]
-    copies = [[None] * 6 for _ in range(6)]
-
-    def densify(p, lo):
-        def body(i, _):
-            for u in range(8):
-                e = lo + i * 8 + u
-                acc[p][e] = own[p][own_idx[p * 128 + e]] + prt[p][prt_idx[p * 128 + e]]
-            return 0
-
-        lax.fori_loop(0, 8, body, 0)
-
-    def add_in(p, at, lo, n):
+    bases = [[None] * 7 for _ in parts]
+    copies = [[None] * 6 for _ in parts]
+
+    def encode(v):
+        size = jnp.max(jnp.abs(v), axis=0, keepdims=True)
+        gain = jnp.where(size > TINY, LEVELS / jnp.maximum(size, TINY), 0.0)
+        code = (v * gain + 32768.5).astype(jnp.int32)
+        return (code[:8] << 16) | code[8:], size
+
+    def decode(word, size):
+        unit = size * (1.0 / LEVELS)
+        high = lax.shift_right_logical(word, 16).astype(jnp.float32)
+        low = (word & 0xFFFF).astype(jnp.float32)
+        return jnp.concatenate([(high - 32768.0) * unit, (low - 32768.0) * unit], axis=0)
+
+    def each(n, fn):
         unroll = min(n, 8)
 
         def body(i, _):
             for u in range(unroll):
-                e = i * unroll + u
-                acc[p][at + e] = acc[p][at + e] + got[p][lo + e]
+                fn(i * unroll + u)
             return 0
 
         lax.fori_loop(0, n // unroll, body, 0)
+
+    def densify(p, lo, to=None):
+        def one(i):
+            e = lo + i
+            v = own[p][own_idx[p * 128 + e]] + prt[p][prt_idx[p * 128 + e]]
+            if to is None:
+                acc[p][e] = v
+            else:
+                out[p][to + i], outs[p][to + i] = encode(v)
+
+        each(64, one)
+
+    def add_in(p, at, lo, n, to=None):
+        def one(i):
+            v = acc[p][at + i] + decode(got[p][lo + i], gots[p][lo + i])
+            if to is None:
+                acc[p][at + i] = v
+            else:
+                out[p][to + i], outs[p][to + i] = encode(v)
+
+        each(n, one)
+
+    def offset(s):
+        return 128 - (128 >> s)
 
     def send(p, s):
         device, bit = across[ORDERS[p][s]]
         half = 64 >> s
-        base = bases[p][s]
-        c = pltpu.make_async_remote_copy(
-            acc[p].at[pl.ds(base + (1 - bit) * half, half)],
-            got[p].at[pl.ds(128 - (128 >> s), half)],
-            cube_send.at[p, s], cube_recv.at[p, s], device_id=device,
-        )
-        c.start()
-        copies[p][s] = c
-        bases[p][s + 1] = base + bit * half
+        region = pl.ds(offset(s), half)
+        both = []
+        for k, (src, dst) in enumerate(((out, got), (outs, gots))):
+            c = pltpu.make_async_remote_copy(
+                src[p].at[region], dst[p].at[region], cube_send.at[k, p, s], cube_recv.at[k, p, s], device_id=device,
+            )
+            c.start()
+            both.append(c)
+        copies[p][s] = both
+        bases[p][s + 1] = bases[p][s] + bit * half
 
     for p in parts:
         own_copies[p].wait()
         d2d_copies[p].wait_recv()
         bases[p][0] = 0
         bit = across[ORDERS[p][0]][1]
-        densify(p, (1 - bit) * 64)
+        densify(p, (1 - bit) * 64, 0)
         send(p, 0)
         densify(p, bit * 64)
 
@@ -260,19 +292,22 @@
         live_copies.append(live_copy(s, lbuf.at[s - 1], across[ORDERS[0][s - 1]][0]))
         live_copies[s].start()
         for p in parts:
-            copies[p][s - 1].wait_recv()
+            for c in copies[p][s - 1]:
+                c.wait_recv()
             half = 64 >> (s - 1)
-            lo = 128 - (128 >> (s - 1))
+            lo = offset(s - 1)
             base = bases[p][s]
             if s < 6:
                 quarter = half // 2
                 bit = across[ORDERS[p][s]][1]
-                add_in(p, base + (1 - bit) * quarter, lo + (1 - bit) * quarter, quarter)
+                away = (1 - bit) * quarter
+                add_in(p, base + away, lo + away, quarter, offset(s))
                 send(p, s)
                 add_in(p, base + bit * quarter, lo + bit * quarter, quarter)
             else:
                 for k in range(2):
-                    sk_out[k, STARTS[p] : STARTS[p] + ROWS[p], :] = acc[p][base + k] + got[p][lo + k]
+                    v = acc[p][base + k] + decode(got[p][lo + k], gots[p][lo + k])
+                    sk_out[k, p * ROWS : (p + 1) * ROWS, :] = v
         live_copies[s].wait_recv()
         lbuf[s] = lbuf[s - 1] + lgot[s]
     live_out[...] = lbuf[6]
@@ -296,10 +331,11 @@
     meta_back.wait()
     for c in live_copies:
         c.wait_send()
-    for p in range(6):
+    for p in parts:
         d2d_copies[p].wait_send()
         for s in range(6):
-            copies[p][s].wait_send()
+            for c in copies[p][s]:
+                c.wait_send()
 
 
 def exchange_call(own_idx, prt_idx, table, stats, meta, live):
@@ -308,10 +344,12 @@
     smem = pl.BlockSpec(memory_space=pltpu.SMEM)
     f32 = jnp.float32
     scratch = (
-        [pltpu.VMEM((BLK + 1, r, LANES), f32) for r in ROWS]
-        + [pltpu.VMEM((BLK + 1, r, LANES), f32) for r in ROWS]
-        + [pltpu.VMEM((128, r, LANES), f32) for r in ROWS]
-        + [pltpu.VMEM((126, r, LANES), f32) for r in ROWS]
+        [pltpu.VMEM((BLK + 1, ROWS, LANES), f32)] * (2 * PARTS)
+        + [pltpu.VMEM((128, ROWS, LANES), f32)] * PARTS
+        + [pltpu.VMEM((126, 8, LANES), jnp.int32)] * PARTS
+        + [pltpu.VMEM((126, 1, LANES), f32)] * PARTS
+        + [pltpu.VMEM((126, 8, LANES), jnp.int32)] * PARTS
+        + [pltpu.VMEM((126, 1, LANES), f32)] * PARTS
         + [
             pltpu.VMEM((CAP, 32, LANES), jnp.bfloat16),
             pltpu.VMEM((1, LANES), f32),
@@ -320,11 +358,11 @@
             pltpu.VMEM((7, 1, LANES), f32),
         ]
         + [
-            pltpu.SemaphoreType.DMA((6,)),
-            pltpu.SemaphoreType.DMA((6,)),
-            pltpu.SemaphoreType.DMA((6,)),
-            pltpu.SemaphoreType.DMA((6, 6)),
-            pltpu.SemaphoreType.DMA((6, 6)),
+            pltpu.SemaphoreType.DMA((PARTS,)),
+            pltpu.SemaphoreType.DMA((PARTS,)),
+            pltpu.SemaphoreType.DMA((PARTS,)),
+            pltpu.SemaphoreType.DMA((2, PARTS, 6)),
+            pltpu.SemaphoreType.DMA((2, PARTS, 6)),
             pltpu.SemaphoreType.DMA((2, SHARDS)),
             pltpu.SemaphoreType.DMA((2, SHARDS)),
             pltpu.SemaphoreType.DMA((7,)),
@@ -374,7 +412,7 @@
 
 
 def finish_call(counts, stats, sketches, live):
-    step = 16
+    step = 32
     return pl.pallas_call(
         functools.partial(finish_kernel, step=step),
         grid=(SHARDS * CAP // step,),

time: 105 us -> 86 us (0.82)
  Pallas kernels: 95.9 us -> 76.9 us
    pallas_call x1, Pallas kernels: 72.4 us -> 55.4 us  [exchange_call(): pl.pallas_call(exchange_kernel, in_specs=[smem, smem, any_, any_, any_, a...]
    pallas_call x1, Pallas kernels: 6.1 us -> 4.15 us  [finish_call(): pl.pallas_call(functools.partial(finish_kernel, step=step), grid=(SHARDS...]
  transfers between devices with their start and end apart: 1 -> 1, of which waited for: 0 -> 0; matrix products, arithmetic and copies ran while one was open for 1% -> 2% of each run, Pallas kernels for 0% -> 0%
where the time goes in v2:
time: 86 us; the launch traced here: 85.4 us
  Pallas kernels  76.9 us (89%)
  other arithmetic  7.65 us (9%)
    pallas_call x1, Pallas kernels, exchange_call(): pl.pallas_call(exchange_kernel, in_specs=[smem, smem, any_, any_, any_, a...  55.4 us
    pallas_call x1, Pallas kernels, local_call(): pl.pallas_call(functools.partial(local_kernel, step=step), grid=(BLK // s...  17.3 us
    pallas_call x1, Pallas kernels, finish_call(): pl.pallas_call(functools.partial(finish_kernel, step=step), grid=(SHARDS...  4.15 us
  transfers between devices with their start and end apart: 1, of which 0 were waited for; matrix products, arithmetic and copies ran while one was open for 2% of the time, Pallas kernels for 0%

profile of v2, /device:TPU:0, one launch (start us, length us, event | category | flops | bytes accessed | tf_op | source)
XLA Modules:
  0.0 85.4 jit_solution(12368396511254913177)
XLA Ops:
  0.6 0.1 collective-permute-start
  0.7 0.7 broadcast_add_fusion
  1.4 0.7 convert_element_type.22
  2.1 0.0 collective-permute-done
  2.1 0.9 %select_reduce_fusion.4 = (s32[64]{0:T(128)S(1)}, s32[64]{0:T(128)S(1)}) fusion(s32[64]{0:T(128)S(1)} %collective-permute-done, s32[256]{0:T(256)} %param.12, s32[64]{0:T(128)} %param.11), kind=kLoop, calls=%fused_computation.4 | loop fusion | flops 98176 | bytes 2048 | tf_op jit(solution)/shard_map/reduce_sum | solution.py:441
  3.0 0.2 convert_reduce_fusion.1
  3.2 0.2 select_reduce_fusion.6
  3.4 0.2 convert_reduce_fusion
  3.6 1.3 %select_reduce_fusion.3 = f32[2,128]{1,0:T(2,128)} fusion(f32[64]{0:T(128)S(1)} %convert_element_type.22, s32[2,128]{1,0:T(2,128)} %constant.83.clone, s32[64]{0:T(128)S(1)} %get-tuple-element.24), kind=kLoop, calls=%fused_computation.3 | loop fusion | flops 48896 | bytes 2560 | tf_op jit(solution)/shard_map/reduce_sum | solution.py:477
  4.9 0.7 select_reduce_fusion.1
  5.7 1.5 %select_reduce_fusion = f32[32,128]{1,0:T(8,128)} fusion(f32[64]{0:T(128)S(1)} %convert_element_type.22, s32[32,128]{1,0:T(8,128)} %constant.84.clone, s32[64]{0:T(128)S(1)} %get-tuple-element.25), kind=kLoop, calls=%fused_computation | loop fusion | flops 782336 | bytes 33280 | tf_op jit(solution)/shard_map/reduce_sum | solution.py:479
  7.2 1.2 %pad_add_fusion.idx_ref = s32[4,64]{1,0:T(4,128)} fusion(s32[1,64]{1,0:T(1,128)} %bitcast.38, s32[1,64]{1,0:T(1,128)S(1)} %get-tuple-element.28, s32[1,64]{1,0:T(1,128)S(1)} %compare_convert_fusion, s32[1,64]{1,0:T(1,128)S(1)} %get-tuple-element.27), kind=kLoop, calls=%fused_computation.14 | loop fusion | flops 768 | bytes 2048 | tf_op jit(solution)/shard_map/stack | solution.py:462
  8.4 17.3 %local_stats.1 = (f32[128,128,128]{2,1,0:T(8,128)}, bf16[128,32,128]{2,1,0:T(8,128)(2,1)}) custom-call(s32[4,64]{1,0:T(4,128)} %pad_add_fusion.idx_ref, bf16[64,480,128]{2,1,0:T(8,128)(2,1)} %samples_ref.1, s32[64,480]{1,0:T(8,128)} %marks_ref.1), custom_call_target="tpu_custom_call" | custom-call | tf_op jit(solution)/shard_map/local_stats/pallas_call | solution.py:92
  25.8 55.4 %exchange.1 = (f32[2,128,128]{2,1,0:T(8,128)}, bf16[32,4,32,128]{3,2,1,0:T(8,128)(2,1)}, f32[32,1,128]{2,1,0:T(1,128)}, f32[1,128]{1,0:T(1,128)}) custom-call(s32[1024]{0:T(1024)} %get-tuple-element.22.own_idx, s32[1024]{0:T(1024)} %get-tuple-element.21.prt_idx, f32[2,64,128,128]{3,2,1,0:T(8,128)} %bitcast.33, bf16[32,4,32,128]{3,2,1,0:T(8,128)(2,1)} %bitcast.35, ...), custom_call_target="tpu_custom_call" | custom-call | tf_op jit(solution)/shard_map/exchange/pallas_call | solution.py:373
  81.2 4.2 %finish.1 = (f32[128,4,8,128]{3,2,1,0:T(8,128)}, f32[2,128,128]{2,1,0:T(8,128)}, f32[2]{0:T(128)}) custom-call(f32[32,1,128]{2,1,0:T(1,128)} %get-tuple-element.14.counts, bf16[128,32,128]{2,1,0:T(8,128)(2,1)} %bitcast.34, f32[2,128,128]{2,1,0:T(8,128)} %get-tuple-element.16.sk_ref, f32[1,128]{1,0:T(1,128)} %get-tuple-element.17.live_ref), custom_call_target="tpu_custom_call" | custom-call | tf_op jit(solution)/shard_map/finish/pallas_call | solution.py:416
  (5 shorter events, 0.1 us)
Async XLA Ops:
  0.6 1.5 %collective-permute-start = (s32[64]{0:T(128)}, s32[64]{0:T(128)S(1)}, u32[]{:S(2)}, u32[]{:S(2)}) collective-permute-start(s32[64]{0:T(128)} %param.11), channel_id=1, source_target_pairs={{0,4},{4,0},{8,12},{12,8},{16,20},{20,16},{24,28},{28,24},{32,36},... | collective-permute-start | bytes 776 | tf_op jit(solution)/shard_map/ppermute | solution.py:455

commit v3 on v2

--- a/solution.py
+++ b/solution.py
@@ -37,77 +37,194 @@
     return table
 
 
-def local_kernel(idx_ref, samples_ref, marks_ref, table_ref, stats_ref, *, step):
-    base = pl.program_id(0) * step
-    rows = lax.broadcasted_iota(jnp.int32, (1, SAMPLES), 1)
+def minute_extremes(x, count):
+    sub16 = lax.broadcasted_iota(jnp.int16, (16, LANES), 0)
+    sub = lax.broadcasted_iota(jnp.int32, (8, LANES), 0)
+    least = jnp.zeros((8, LANES), jnp.float32)
+    most = jnp.zeros((8, LANES), jnp.float32)
+    inf = jnp.bfloat16(jnp.inf)
+    for q in range(2):
+        lo = [None] * 4
+        hi = [None] * 4
+        for v in range(15):
+            at_row = 240 * q + 16 * v
+            val = x[at_row : at_row + 16]
+            ok = sub16 < jnp.full((16, LANES), jnp.clip(count - at_row, 0, 16), jnp.int32).astype(jnp.int16)
+            small, large = jnp.where(ok, val, inf), jnp.where(ok, val, -inf)
+            for h in range(4):
+                a, b = 60 * h - 16 * v, 60 * h + 60 - 16 * v
+                if b <= 0 or a >= 16:
+                    continue
+                s, g = small, large
+                if a > 0:
+                    s, g = jnp.where(sub16 >= a, s, inf), jnp.where(sub16 >= a, g, -inf)
+                if b < 16:
+                    s, g = jnp.where(sub16 < b, s, inf), jnp.where(sub16 < b, g, -inf)
+                lo[h] = s if lo[h] is None else jnp.minimum(lo[h], s)
+                hi[h] = g if hi[h] is None else jnp.maximum(hi[h], g)
+        for h in range(4):
+            m = 4 * q + h
+            least = jnp.where(sub == m, jnp.min(lo[h].astype(jnp.float32), axis=0, keepdims=True), least)
+            most = jnp.where(sub == m, jnp.max(hi[h].astype(jnp.float32), axis=0, keepdims=True), most)
+    return least.astype(jnp.bfloat16), most.astype(jnp.bfloat16)
+
+
+def iota(shape, dim):
+    return lax.broadcasted_iota(jnp.int32, shape, dim).astype(jnp.float32)
+
+
+def routing(series_row, map_row):
+    sub, lane = iota((BLK, BLK), 0), iota((BLK, BLK), 1)
+    eye = sub == lane
+
+    def row(col):
+        return jnp.sum(jnp.where(eye, col, 0.0), axis=0, keepdims=True)
+
+    series = jnp.sum(jnp.where(eye, series_row, 0.0), axis=1, keepdims=True)
+    pos = jnp.sum(jnp.where(iota((BLK, 256), 1) == series, map_row, 0.0), axis=1, keepdims=True)
+    owner = jnp.floor(pos * 0.125)
+    pos_r, owner_r = row(pos), row(owner)
+    rank = jnp.sum(jnp.where((owner == owner_r) & (lane < sub), 1.0, 0.0), axis=1, keepdims=True)
+    slot = jnp.floor(owner * 0.5) * CAP + rank
+    return pos, owner, rank, slot, pos_r, owner_r, row(rank), row(slot)
+
+
+def local_kernel(
+    samples, marks_ref, counts_ref, series_ref, theirs_ref, map_ref, target_ref, live_at,
+    table, stats, own_out, prt_out, meta_out, live_out,
+    x_buf, t_buf, st_buf, idx_v, idx_ref, in_sem, t_sem, st_sem, idx_sem,
+    *, step,
+):
+    steps = BLK // step
+    for i in range(steps):
+        part = pl.ds(i * step, step)
+        pltpu.make_async_copy(samples.at[part], x_buf.at[part], in_sem.at[i]).start()
+
+    map_row = map_ref[...].astype(jnp.float32)
+    counts_row = counts_ref[...].astype(jnp.float32)
+    pos, owner, rank, slot, pos_r, owner_r, rank_r, slot_r = routing(series_ref[...].astype(jnp.float32), map_row)
+    sub, lane = iota((BLK, BLK), 0), iota((BLK, BLK), 1)
+    same = pos == pos_r
+    first = jnp.min(jnp.where(same, slot, 1000.0), axis=0, keepdims=True)
+    later = jnp.max(jnp.where(same & (sub > lane), 1.0, 0.0), axis=0, keepdims=True)
+    odd = owner_r - 2.0 * jnp.floor(owner_r * 0.5)
+    rows = (
+        odd * BLK + first,
+        jnp.where(first == slot_r, 1.0, 0.0),
+        owner_r * CAP + rank_r,
+        counts_row,
+        1.0 - later,
+    )
+    for r, value in enumerate(rows):
+        idx_v[r : r + 1, 0:BLK] = value.astype(jnp.int32)
+    idx_copy = pltpu.make_async_copy(idx_v, idx_ref, idx_sem)
+    idx_copy.start()
+    core = lax.rem(lax.axis_index("shard"), 2)
+    their = routing(theirs_ref[...].astype(jnp.float32), map_row)
+    for p in range(PARTS):
+        want = (target_ref[p : p + 1, :] + core * 8).astype(jnp.float32)
+        for out, (at, val) in ((own_out, (pos, slot)), (prt_out, (their[0], their[3]))):
+            hit = jnp.min(jnp.where(at == want, val, float(BLK)), axis=0, keepdims=True)
+            out[p : p + 1, :] = hit.astype(jnp.int32)
+    counts_col = jnp.sum(jnp.where(sub == lane, counts_row, 0.0), axis=1, keepdims=True)
+    for r in range(2):
+        at = live_at[r : r + 1, :].astype(jnp.float32)
+        live_out[r] = jnp.sum(jnp.where(pos == at, counts_col, 0.0), axis=0, keepdims=True)
+    pick = jnp.where(iota((SHARDS, BLK), 0) == owner_r, 1.0, 0.0)
+    put = jnp.where(iota((BLK, LANES), 1) == rank, counts_col, 0.0)
+    meta = jnp.dot(pick, put, precision=lax.Precision.HIGHEST, preferred_element_type=jnp.float32)
+    for o in range(SHARDS):
+        meta_out[o] = meta[o : o + 1, :]
+    idx_copy.wait()
+
+    row_at = lax.broadcasted_iota(jnp.int32, (1, SAMPLES), 1)
     bins = lax.broadcasted_iota(jnp.int32, (BINS, SAMPLES), 0)
     first_row = lax.broadcasted_iota(jnp.int32, (16, SAMPLES), 0) * 60
-    sub = lax.broadcasted_iota(jnp.int32, (8, LANES), 0)
-    for j in range(step):
-        b = base + j
-        slot, fresh, place, count = idx_ref[0, b], idx_ref[1, b], idx_ref[2, b], idx_ref[3, b]
-        x = samples_ref[j]
-        live = rows < count
-        marks = jnp.where(live, marks_ref[pl.ds(b, 1), :], -1)
-        hot = jnp.where(bins == marks, 1.0, 0.0).astype(jnp.bfloat16)
-        at = jnp.where(live, rows, -1)
-        minute = jnp.where((at >= first_row) & (at < first_row + 60), 1.0, 0.0).astype(jnp.bfloat16)
-        both = jnp.dot(jnp.concatenate([hot, minute], axis=0), x, preferred_element_type=jnp.float32)
-        old = table_ref[slot]
-        table_ref[slot] = jnp.where(fresh == 1, 0.0, old) + both[:BINS]
-        total = both[BINS : BINS + 8]
-        high = total.astype(jnp.bfloat16)
-        low = (total - high.astype(jnp.float32)).astype(jnp.bfloat16)
-        least = jnp.zeros((8, LANES), jnp.float32)
-        most = jnp.zeros((8, LANES), jnp.float32)
-        for q in range(4):
-            lo = [None, None]
-            hi = [None, None]
-            for v in range(15):
-                at_row = 120 * q + 8 * v
-                val = x[at_row : at_row + 8].astype(jnp.float32)
-                ok = sub < count - at_row
-                small = jnp.where(ok, val, jnp.inf)
-                large = jnp.where(ok, val, -jnp.inf)
-                for h in (0, 1):
-                    if (h == 0 and v > 7) or (h == 1 and v < 7):
-                        continue
-                    s, g = small, large
-                    if v == 7:
-                        mine = (sub < 4) if h == 0 else (sub >= 4)
-                        s, g = jnp.where(mine, s, jnp.inf), jnp.where(mine, g, -jnp.inf)
-                    lo[h] = s if lo[h] is None else jnp.minimum(lo[h], s)
-                    hi[h] = g if hi[h] is None else jnp.maximum(hi[h], g)
-            for h in (0, 1):
-                m = 2 * q + h
-                least = jnp.where(sub == m, jnp.min(lo[h], axis=0, keepdims=True), least)
-                most = jnp.where(sub == m, jnp.max(hi[h], axis=0, keepdims=True), most)
-        stats_ref[place] = jnp.concatenate(
-            [least.astype(jnp.bfloat16), most.astype(jnp.bfloat16), high, low], axis=0
-        )
-
-
-def local_call(idx, samples, marks):
-    step = 4
+
+    def t_copy(b):
+        at = idx_ref[0, b]
+        return pltpu.make_async_copy(t_buf.at[at], table.at[at], t_sem.at[b])
+
+    def st_copy(b):
+        return pltpu.make_async_copy(st_buf.at[b], stats.at[idx_ref[2, b]], st_sem.at[b])
+
+    def chunk(i, _):
+        part = pl.ds(i * step, step)
+        pltpu.make_async_copy(samples.at[part], x_buf.at[part], in_sem.at[i]).wait()
+        for j in range(step):
+            b = i * step + j
+            slot_b, fresh, count, last = idx_ref[0, b], idx_ref[1, b], idx_ref[3, b], idx_ref[4, b]
+            x = x_buf[b]
+            live = row_at < count
+            marks = jnp.where(live, marks_ref[pl.ds(b, 1), :], -1)
+            hot = jnp.where(bins == marks, 1.0, 0.0).astype(jnp.bfloat16)
+            at = jnp.where(live, row_at, -1)
+            minute = jnp.where((at >= first_row) & (at < first_row + 60), 1.0, 0.0).astype(jnp.bfloat16)
+            both = jnp.dot(jnp.concatenate([hot, minute], axis=0), x, preferred_element_type=jnp.float32)
+            t_buf[slot_b] = jnp.where(fresh == 1, 0.0, t_buf[slot_b]) + both[:BINS]
+            total = both[BINS : BINS + 8]
+            high = total.astype(jnp.bfloat16)
+            low = (total - high.astype(jnp.float32)).astype(jnp.bfloat16)
+            least, most = minute_extremes(x, count)
+            st_buf[b] = jnp.concatenate([least, most, high, low], axis=0)
+            st_copy(b).start()
+
+            @pl.when(last == 1)
+            def _():
+                t_copy(b).start()
+
+        return 0
+
+    lax.fori_loop(0, steps, chunk, 0)
+
+    def finish(b, _):
+        st_copy(b).wait()
+
+        @pl.when(idx_ref[4, b] == 1)
+        def _():
+            t_copy(b).wait()
+
+        return 0
+
+    lax.fori_loop(0, BLK, finish, 0)
+
+
+def local_call(samples, marks, counts, series, theirs, owner_map):
+    step = 8
+    vmem = pl.BlockSpec(memory_space=pltpu.VMEM)
+    any_ = pl.BlockSpec(memory_space=pl.ANY)
+    lane = np.arange(LANES)
+    live_at = np.stack([(lane // 8) * 16 + r * 8 + lane % 8 for r in (0, 1)]).astype(np.int32)
+    i32, f32 = jnp.int32, jnp.float32
     return pl.pallas_call(
         functools.partial(local_kernel, step=step),
-        grid=(BLK // step,),
-        in_specs=[
-            pl.BlockSpec(memory_space=pltpu.SMEM),
-            pl.BlockSpec((step, SAMPLES, LANES), lambda i: (i, 0, 0)),
-            pl.BlockSpec((BLK, SAMPLES), lambda i: (0, 0)),
+        in_specs=[any_] + [vmem] * 7,
+        out_specs=[any_, any_] + [vmem] * 4,
+        out_shape=[
+            jax.ShapeDtypeStruct((SHARDS * CAP, BINS, LANES), f32),
+            jax.ShapeDtypeStruct((SHARDS * CAP, 32, LANES), jnp.bfloat16),
+            jax.ShapeDtypeStruct((PARTS, 128), i32),
+            jax.ShapeDtypeStruct((PARTS, 128), i32),
+            jax.ShapeDtypeStruct((SHARDS, 1, LANES), f32),
+            jax.ShapeDtypeStruct((2, 1, LANES), f32),
         ],
-        out_specs=[
-            pl.BlockSpec((SHARDS * CAP, BINS, LANES), lambda i: (0, 0, 0)),
-            pl.BlockSpec((SHARDS * CAP, 32, LANES), lambda i: (0, 0, 0)),
-        ],
-        out_shape=[
-            jax.ShapeDtypeStruct((SHARDS * CAP, BINS, LANES), jnp.float32),
-            jax.ShapeDtypeStruct((SHARDS * CAP, 32, LANES), jnp.bfloat16),
+        scratch_shapes=[
+            pltpu.VMEM((BLK, SAMPLES, LANES), jnp.bfloat16),
+            pltpu.VMEM((SHARDS * CAP, BINS, LANES), f32),
+            pltpu.VMEM((BLK, 32, LANES), jnp.bfloat16),
+            pltpu.VMEM((8, 128), i32),
+            pltpu.SMEM((8, 128), i32),
+            pltpu.SemaphoreType.DMA((BLK // step,)),
+            pltpu.SemaphoreType.DMA((BLK,)),
+            pltpu.SemaphoreType.DMA((BLK,)),
+            pltpu.SemaphoreType.DMA,
         ],
         compiler_params=pltpu.CompilerParams(vmem_limit_bytes=56 * 2**20),
         name="local_stats",
-    )(idx, samples, marks)
+    )(
+        samples, marks, counts.reshape(1, BLK), series.reshape(1, BLK), theirs.reshape(1, BLK),
+        owner_map.reshape(1, -1), jnp.asarray(part_positions()), jnp.asarray(live_at),
+    )
 
 
 def exchange_kernel(
@@ -242,7 +359,7 @@
     def densify(p, lo, to=None):
         def one(i):
             e = lo + i
-            v = own[p][own_idx[p * 128 + e]] + prt[p][prt_idx[p * 128 + e]]
+            v = own[p][own_idx[p, e]] + prt[p][prt_idx[p, e]]
             if to is None:
                 acc[p][e] = v
             else:
@@ -388,99 +505,71 @@
     )(own_idx, prt_idx, table, stats, meta, live)
 
 
-def finish_kernel(counts, stats_ref, sk_ref, live_ref, cold_ref, sk_out, live_out, *, step):
-    i = pl.program_id(0)
+def finish_kernel(counts, stats, sk_ref, live_ref, cold, sk_out, live_out, st_buf, cold_buf, in_sem, out_sem, *, step):
+    steps = SHARDS * CAP // step
+    for i in range(steps):
+        part = pl.ds(i * step, step)
+        pltpu.make_async_copy(stats.at[part], st_buf.at[part], in_sem.at[i]).start()
     minute = lax.broadcasted_iota(jnp.int32, (8, LANES), 0).astype(jnp.float32) * 60.0
-    for j in range(step):
-        at = i * step + j
-        n = counts[lax.div(at, CAP), 0, lax.rem(at, CAP)]
-        count = jnp.clip(n - minute, 0.0, 60.0)
-        filled = count > 0
-        st = stats_ref[j].astype(jnp.float32)
-        cold_ref[j, 0] = jnp.where(filled, st[0:8], 0.0)
-        cold_ref[j, 1] = jnp.where(filled, st[8:16], 0.0)
-        cold_ref[j, 2] = jnp.where(filled, st[16:24] + st[24:32], 0.0)
-        cold_ref[j, 3] = count
-
-    @pl.when(i == 0)
-    def _():
-        sk_out[...] = sk_ref[...]
-        at = lax.div(lax.axis_index("shard"), 2) * 8 + lax.axis_index("replica") * 2
-        lane = lax.broadcasted_iota(jnp.int32, (1, LANES), 1)
-        for k in range(2):
-            live_out[k] = jnp.sum(jnp.where(lane == at + k, live_ref[...], 0.0))
+    sk_out[...] = sk_ref[...]
+    place = lax.div(lax.axis_index("shard"), 2) * 8 + lax.axis_index("replica") * 2
+    lane = lax.broadcasted_iota(jnp.int32, (1, LANES), 1)
+    for k in range(2):
+        live_out[k] = jnp.sum(jnp.where(lane == place + k, live_ref[...], 0.0))
+    for i in range(steps):
+        part = pl.ds(i * step, step)
+        pltpu.make_async_copy(stats.at[part], st_buf.at[part], in_sem.at[i]).wait()
+
+        def group(g, _):
+            source = i * (step // CAP) + g
+            for c in range(CAP):
+                at = source * CAP + c
+                count = jnp.clip(counts[source, 0, c] - minute, 0.0, 60.0)
+                filled = count > 0
+                st = st_buf[at].astype(jnp.float32)
+                cold_buf[at, 0] = jnp.where(filled, st[0:8], 0.0)
+                cold_buf[at, 1] = jnp.where(filled, st[8:16], 0.0)
+                cold_buf[at, 2] = jnp.where(filled, st[16:24] + st[24:32], 0.0)
+                cold_buf[at, 3] = count
+            return 0
+
+        lax.fori_loop(0, step // CAP, group, 0)
+        pltpu.make_async_copy(cold_buf.at[part], cold.at[part], out_sem.at[i]).start()
+    for i in range(steps):
+        part = pl.ds(i * step, step)
+        pltpu.make_async_copy(cold_buf.at[part], cold.at[part], out_sem.at[i]).wait()
 
 
 def finish_call(counts, stats, sketches, live):
     step = 32
+    vmem = pl.BlockSpec(memory_space=pltpu.VMEM)
+    smem = pl.BlockSpec(memory_space=pltpu.SMEM)
+    any_ = pl.BlockSpec(memory_space=pl.ANY)
     return pl.pallas_call(
         functools.partial(finish_kernel, step=step),
-        grid=(SHARDS * CAP // step,),
-        in_specs=[
-            pl.BlockSpec(memory_space=pltpu.SMEM),
-            pl.BlockSpec((step, 32, LANES), lambda i: (i, 0, 0)),
-            pl.BlockSpec((2, BINS, LANES), lambda i: (0, 0, 0)),
-            pl.BlockSpec((1, LANES), lambda i: (0, 0)),
-        ],
-        out_specs=[
-            pl.BlockSpec((step, 4, 8, LANES), lambda i: (i, 0, 0, 0)),
-            pl.BlockSpec((2, BINS, LANES), lambda i: (0, 0, 0)),
-            pl.BlockSpec(memory_space=pltpu.SMEM),
-        ],
+        in_specs=[smem, any_, vmem, vmem],
+        out_specs=[any_, vmem, smem],
         out_shape=[
             jax.ShapeDtypeStruct((SHARDS * CAP, 4, 8, LANES), jnp.float32),
             jax.ShapeDtypeStruct((2, BINS, LANES), jnp.float32),
             jax.ShapeDtypeStruct((2,), jnp.float32),
         ],
+        scratch_shapes=[
+            pltpu.VMEM((SHARDS * CAP, 32, LANES), jnp.bfloat16),
+            pltpu.VMEM((SHARDS * CAP, 4, 8, LANES), jnp.float32),
+            pltpu.SemaphoreType.DMA((SHARDS * CAP // step,)),
+            pltpu.SemaphoreType.DMA((SHARDS * CAP // step,)),
+        ],
         name="finish",
     )(counts, stats, sketches, live)
 
 
-def positions_of(block_series, owner_map):
-    series = jnp.arange(owner_map.shape[0], dtype=jnp.int32)
-    return jnp.sum(jnp.where(block_series[:, None] == series[None, :], owner_map[None, :], 0), axis=1)
-
-
-def slots_of(position):
-    owner = position // 8
-    index = jnp.arange(BLK, dtype=jnp.int32)
-    earlier = index[None, :] < index[:, None]
-    rank = jnp.sum(((owner[:, None] == owner[None, :]) & earlier).astype(jnp.int32), axis=1)
-    return owner, rank, (owner // 2) * CAP + rank
-
-
 def body(samples, counts, buckets, block_series, owner_map):
-    core = lax.axis_index("shard") % 2
     swap = [(i, i ^ 1) for i in range(SHARDS)]
-    their_series = lax.ppermute(block_series, "shard", swap)
-    position = positions_of(block_series, owner_map)
-    owner, rank, half_slot = slots_of(position)
-    same = position[:, None] == position[None, :]
-    first_slot = jnp.min(jnp.where(same, half_slot[None, :], 2 * BLK), axis=1)
-    fresh = (first_slot == half_slot).astype(jnp.int32)
-    place = owner * CAP + rank
-    idx = jnp.stack([(owner % 2) * BLK + first_slot, fresh, place, counts])
-    table, stats = local_call(idx, samples, buckets)
-
-    target = jnp.asarray(part_positions().reshape(-1)) + core * 8
-
-    def entries(pos, slot):
-        hit = target[:, None] == pos[None, :]
-        return jnp.min(jnp.where(hit, slot[None, :], BLK), axis=1)
-
-    own_idx = entries(position, half_slot)
-    their_position = positions_of(their_series, owner_map)
-    prt_idx = entries(their_position, slots_of(their_position)[2])
-    rows = counts.astype(jnp.float32)
-    lane = np.arange(128)
-    live_at = jnp.asarray(np.stack([(lane // 8) * 16 + r * 8 + lane % 8 for r in (0, 1)]).astype(np.int32))
-    live = jnp.sum(jnp.where(live_at[:, :, None] == position[None, None, :], rows[None, None, :], 0.0), axis=2)
-    at = np.where(lane[None, :] < CAP, np.arange(SHARDS)[:, None] * CAP + lane[None, :], -1).astype(np.int32)
-    meta = jnp.sum(jnp.where(jnp.asarray(at)[:, :, None] == place[None, None, :], rows[None, None, :], 0.0), axis=2)
+    theirs = lax.ppermute(block_series, "shard", swap)
+    table, stats, own_idx, prt_idx, meta, live = local_call(samples, buckets, counts, block_series, theirs, owner_map)
     sk, st, got_counts, got_live = exchange_call(
-        own_idx, prt_idx,
-        table.reshape(2, BLK, BINS, LANES), stats.reshape(SHARDS, CAP, 32, LANES),
-        meta.reshape(SHARDS, 1, LANES), live.reshape(2, 1, LANES),
+        own_idx, prt_idx, table.reshape(2, BLK, BINS, LANES), stats.reshape(SHARDS, CAP, 32, LANES), meta, live,
     )
     cold, sketches, live_rows = finish_call(got_counts, st.reshape(SHARDS * CAP, 32, LANES), sk, got_live)
     return cold.reshape(1, 1, SHARDS * CAP, 4, 8, LANES), sketches, live_rows

time: 86 us -> 74.2 us (0.86)
  other arithmetic: 7.65 us -> 0 us
  Pallas kernels: 76.9 us -> 71.4 us
  waiting for transfers between devices: 0.01 us -> 1.28 us
    pallas_call x2, Pallas kernels: 21.5 us -> 16 us  [the longest x1 12 us: local_call(): pl.pallas_call(functools.partial(local_kernel, step=step), in_specs=[any_...]
    reduce_sum x5 -> x0, other arithmetic: 4.05 us -> none  [the longest x1 1.52 us: body(): jnp.sum(jnp.where(jnp.asarray(at)[:, :, None] == place[None, None, :], ro...]
    ppermute x1, waiting for transfers between devices: 0.01 us -> 1.28 us  [body(): theirs = lax.ppermute(block_series, 'shard', swap)]
    another operation x1 -> x0, other arithmetic: 1.24 us -> none  [body(): idx = jnp.stack([owner % 2 * BLK + first_slot, fresh, place, counts])]
    reduce_min x2 -> x0, other arithmetic: 0.93 us -> none  [the longest x1 0.75 us: entries(): return jnp.min(jnp.where(hit, slot[None, :], BLK), axis=1)]
  transfers between devices with their start and end apart: 1 -> 1, of which waited for: 0 -> 1; matrix products, arithmetic and copies ran while one was open for 2% -> 0% of each run, Pallas kernels for 0% -> 0%
where the time goes in v3:
time: 74.2 us; the launch traced here: 74 us
  Pallas kernels  71.4 us (96%)
  waiting for transfers between devices  1.28 us (2%)
    pallas_call x1, Pallas kernels, exchange_call(): pl.pallas_call(exchange_kernel, in_specs=[smem, smem, any_, any_, any_, a...  55.4 us
    pallas_call x1, Pallas kernels, local_call(): pl.pallas_call(functools.partial(local_kernel, step=step), in_specs=[any_...  12 us
    pallas_call x1, Pallas kernels, finish_call(): pl.pallas_call(functools.partial(finish_kernel, step=step), in_specs=[sme...  4.02 us
  transfers between devices with their start and end apart: 1, of which 1 were waited for; matrix products, arithmetic and copies ran while one was open for 0% of the time, Pallas kernels for 0%

profile of v3, /device:TPU:0, one launch (start us, length us, event | category | flops | bytes accessed | tf_op | source)
XLA Modules:
  0.0 74.0 jit_solution(8627818570296781568)
XLA Ops:
  0.6 0.1 collective-permute-start
  0.7 1.3 %collective-permute-done = s32[64]{0:T(128)S(1)} collective-permute-done((s32[64]{0:T(128)}, s32[64]{0:T(128)S(1)}, u32[]{:S(2)}, u32[]{:S(2)}) %collective-permute-start) | collective-permute-done | bytes 288 | tf_op jit(solution)/shard_map/ppermute | solution.py:569
  2.0 0.0 copy-start
  2.0 0.5 copy-done
  2.5 12.0 %local_stats.1 = (f32[128,128,128]{2,1,0:T(8,128)}, bf16[128,32,128]{2,1,0:T(8,128)(2,1)}, s32[8,128]{1,0:T(8,128)}, s32[8,128]{1,0:T(8,128)}, f32[32,1,128]{2,1,0:T(1,128)}, /*index=5*/f32[2,1,128]{2,1,0:T(1,128)}) custom-call(bf16[64,480,128]{2,1,0:T(8,128)(2,1)} %samples.1, s32[64,480]{1,0:T(8,128)} %marks_ref.1, s32[1,64]{1,0:T(1,128)} %bitcast.12, ...), custom_call_target="tpu_custom_call" | custom-call | tf_op jit(solution)/shard_map/local_stats/pallas_call | solution.py:199
  14.5 55.4 %exchange.1 = (f32[2,128,128]{2,1,0:T(8,128)}, bf16[32,4,32,128]{3,2,1,0:T(8,128)(2,1)}, f32[32,1,128]{2,1,0:T(1,128)}, f32[1,128]{1,0:T(1,128)}) custom-call(s32[8,128]{1,0:T(8,128)} %get-tuple-element.16.own_idx, s32[8,128]{1,0:T(8,128)} %get-tuple-element.17.prt_idx, f32[2,64,128,128]{3,2,1,0:T(8,128)} %bitcast.8, bf16[32,4,32,128]{3,2,1,0:T(8,128)(2,1)} %bitcast.10, ...), custom_call_target="tpu_custom_call" | custom-call | tf_op jit(solution)/shard_map/exchange/pallas_call | solution.py:490
  70.0 4.0 %finish.1 = (f32[128,4,8,128]{3,2,1,0:T(8,128)}, f32[2,128,128]{2,1,0:T(8,128)}, f32[2]{0:T(128)}) custom-call(f32[32,1,128]{2,1,0:T(1,128)} %get-tuple-element.22.counts, bf16[128,32,128]{2,1,0:T(8,128)(2,1)} %bitcast.9, f32[2,128,128]{2,1,0:T(8,128)} %get-tuple-element.24.sk_ref, f32[1,128]{1,0:T(1,128)} %get-tuple-element.25.live_ref), custom_call_target="tpu_custom_call" | custom-call | tf_op jit(solution)/shard_map/finish/pallas_call | solution.py:548
Async XLA Ops:
  0.6 1.4 %collective-permute-start = (s32[64]{0:T(128)}, s32[64]{0:T(128)S(1)}, u32[]{:S(2)}, u32[]{:S(2)}) collective-permute-start(s32[64]{0:T(128)} %param.10), channel_id=1, source_target_pairs={{0,4},{4,0},{8,12},{12,8},{16,20},{20,16},{24,28},{28,24},{32,36},... | collective-permute-start | bytes 776 | tf_op jit(solution)/shard_map/ppermute | solution.py:569
  2.0 0.5 copy-start

commit v4 on v3

v4 whole, which is shorter than its diff:
```python
import functools

import jax
import jax.numpy as jnp
import numpy as np
from jax import lax
from jax.experimental import pallas as pl
from jax.experimental.pallas import tpu as pltpu
from jax.sharding import PartitionSpec as P

BINS = 128
LANES = 128
SAMPLES = 480
BLK = 64
SHARDS = 32
REPLICAS = 4
CAP = 4
DIMS = (("x", 0), ("z", 0), ("y", 0), ("x", 1), ("z", 1), ("y", 1))
ORDERS = (
    (5, 2, 4, 0, 3, 1), (5, 4, 1, 2, 0, 3), (2, 5, 1, 3, 4, 0), (0, 1, 4, 3, 5, 2),
    (2, 0, 3, 4, 1, 5), (3, 2, 5, 4, 1, 0), (4, 3, 0, 5, 2, 1), (1, 5, 2, 0, 3, 4),
)
PARTS = len(ORDERS)
ROWS = BINS // PARTS
LEVELS = 32766.0
TINY = 1e-33
GRAY = {(0, 0): 0, (0, 1): 1, (1, 1): 2, (1, 0): 3}


HALVINGS = 3


def last_groups(p):
    tail = ORDERS[p][HALVINGS:]
    return [tuple(d for k, d in enumerate(tail) if m >> k & 1) for m in range(1, 8)]


def off_plane():
    dims = {(order[s],) for order in ORDERS for s in range(HALVINGS)}
    dims |= {tuple(sorted(g)) for p in range(PARTS) for g in last_groups(p)}
    return tuple(sorted(g for g in dims if any(DIMS[d][0] == "y" for d in g)))


OFF_PLANE = off_plane()


def part_positions():
    table = np.zeros((PARTS, 128), np.int32)
    for p, order in enumerate(ORDERS):
        for i in range(128):
            bits = {DIMS[d]: (i >> (6 - s)) & 1 for s, d in enumerate(order)}
            x, y, z = (GRAY[(bits[(a, 1)], bits[(a, 0)])] for a in "xyz")
            table[p, i] = (z * 4 + x) * 16 + y * 2 + (i & 1)
    return table


def minute_extremes(x, count):
    sub16 = lax.broadcasted_iota(jnp.int16, (16, LANES), 0)
    sub = lax.broadcasted_iota(jnp.int32, (8, LANES), 0)
    least = jnp.zeros((8, LANES), jnp.float32)
    most = jnp.zeros((8, LANES), jnp.float32)
    inf = jnp.bfloat16(jnp.inf)
    for q in range(2):
        lo = [None] * 4
        hi = [None] * 4
        for v in range(15):
            at_row = 240 * q + 16 * v
            val = x[at_row : at_row + 16]
            ok = sub16 < jnp.full((16, LANES), jnp.clip(count - at_row, 0, 16), jnp.int32).astype(jnp.int16)
            small, large = jnp.where(ok, val, inf), jnp.where(ok, val, -inf)
            for h in range(4):
                a, b = 60 * h - 16 * v, 60 * h + 60 - 16 * v
                if b <= 0 or a >= 16:
                    continue
                s, g = small, large
                if a > 0:
                    s, g = jnp.where(sub16 >= a, s, inf), jnp.where(sub16 >= a, g, -inf)
                if b < 16:
                    s, g = jnp.where(sub16 < b, s, inf), jnp.where(sub16 < b, g, -inf)
                lo[h] = s if lo[h] is None else jnp.minimum(lo[h], s)
                hi[h] = g if hi[h] is None else jnp.maximum(hi[h], g)
        for h in range(4):
            m = 4 * q + h
            least = jnp.where(sub == m, jnp.min(lo[h].astype(jnp.float32), axis=0, keepdims=True), least)
            most = jnp.where(sub == m, jnp.max(hi[h].astype(jnp.float32), axis=0, keepdims=True), most)
    return least.astype(jnp.bfloat16), most.astype(jnp.bfloat16)


def iota(shape, dim):
    return lax.broadcasted_iota(jnp.int32, shape, dim)


def routing(series_row, map_row):
    sub, lane = iota((BLK, BLK), 0), iota((BLK, BLK), 1)
    eye = sub == lane

    def row(col):
        return jnp.sum(jnp.where(eye, col, 0), axis=0, keepdims=True)

    series = jnp.sum(jnp.where(eye, series_row, 0), axis=1, keepdims=True)
    pos = jnp.sum(jnp.where(iota((BLK, 256), 1) == series, map_row, 0), axis=1, keepdims=True)
    pos_r = row(pos)
    owner, owner_r = pos >> 3, pos_r >> 3
    rank = jnp.sum(jnp.where((owner == owner_r) & (lane < sub), 1, 0), axis=1, keepdims=True)
    return pos, owner, rank, pos_r, owner_r


def flip(v, bit):
    return v + 1 - 2 * lax.rem(v, 2) if bit == 0 else 3 - v


def exchange_kernel(
    samples, marks_ref, counts_ref, series_ref, theirs_ref, map_ref, target_ref, live_at,
    sk_out, stats_out, meta_out, live_out,
    x_buf, own, prt, st_nat, st_slots, meta_v, live_v, idx_v, idx_ref, lbuf, lgot,
    in_sem, idx_sem, d2d_send, d2d_recv, cube_send, cube_recv, st_send, st_recv, l_send, l_recv, loc_sem,
    *rest, step,
):
    acc, out, outs, got, gots = (rest[PARTS * i : PARTS * (i + 1)] for i in range(5))
    steps = BLK // step
    parts = tuple(range(PARTS))

    def in_copy(i):
        part = pl.ds(i * step, step)
        return pltpu.make_async_copy(samples.at[part], x_buf.at[part], in_sem.at[i])

    for i in range(steps):
        in_copy(i).start()

    shard = lax.axis_index("shard")
    y = lax.axis_index("replica")
    core = lax.rem(shard, 2)
    x = lax.rem(lax.div(shard, 2), 4)
    z = lax.div(shard, 8)

    def across(dims):
        v = {"x": x, "y": y, "z": z}
        for d in dims:
            axis, bit = DIMS[d]
            v[axis] = flip(v[axis], bit)
        return {"shard": v["z"] * 8 + v["x"] * 2 + core, "replica": v["y"]}

    def bit_of(d):
        axis, bit = DIMS[d]
        v = {"x": x, "y": y, "z": z}[axis]
        high = lax.div(v, 2)
        return high if bit == 1 else lax.rem(v + high, 2)

    bits = [bit_of(d) for d in range(6)]
    partner = {"shard": shard + 1 - 2 * core, "replica": y}

    barrier = pltpu.get_barrier_semaphore()

    def greet(d, _):
        pl.semaphore_signal(barrier, inc=1, device_id={"shard": lax.rem(shard + d, SHARDS), "replica": y})
        return 0

    lax.fori_loop(1, SHARDS, greet, 0)
    for dims in OFF_PLANE:
        pl.semaphore_signal(barrier, inc=1, device_id=across(dims))

    map_row = map_ref[...]
    pos, owner, rank, pos_r, owner_r = routing(series_ref[...], map_row)
    sub, lane = iota((BLK, BLK), 0), iota((BLK, BLK), 1)
    before = jnp.max(jnp.where((pos == pos_r) & (sub < lane), sub, -1), axis=0, keepdims=True)
    idx_v[0:1, 0:BLK] = jnp.where(before < 0, BLK, jnp.minimum(before, BLK))
    idx_v[1:2, 0:BLK] = counts_ref[...]
    block = iota((BLK, LANES), 0)
    filled = iota((BLK, LANES), 1) == owner * CAP + rank
    idx_v[2:3, :] = jnp.clip(jnp.max(jnp.where(filled, block, 0), axis=0, keepdims=True), 0, BLK - 1)
    their_pos = routing(theirs_ref[...], map_row)[0]
    for p in parts:
        want = target_ref[p : p + 1, :] + core * 8
        for k, at in enumerate((pos, their_pos)):
            hit = jnp.max(jnp.where(at == want, block, -1), axis=0, keepdims=True)
            row = 8 + k * PARTS + p
            idx_v[row : row + 1, :] = jnp.where(hit < 0, BLK, jnp.minimum(hit, BLK))
    idx_copy = pltpu.make_async_copy(idx_v, idx_ref, idx_sem)
    idx_copy.start()
    counts_row = counts_ref[...].astype(jnp.float32)
    counts_col = jnp.sum(jnp.where(sub == lane, counts_row, 0.0), axis=1, keepdims=True)
    for r in range(2):
        at = live_at[r : r + 1, :]
        live_v[r] = jnp.sum(jnp.where(pos == at, counts_col, 0.0), axis=0, keepdims=True)
    pick = jnp.where(iota((SHARDS, BLK), 0) == owner_r, 1.0, 0.0)
    put = jnp.where(iota((BLK, LANES), 1) == rank, counts_col, 0.0)
    meta = jnp.dot(pick, put, precision=lax.Precision.HIGHEST, preferred_element_type=jnp.float32)
    for o in range(SHARDS):
        meta_v[o] = meta[o : o + 1, :]
    own[BLK] = jnp.zeros((BINS, LANES), jnp.float32)
    prt[BLK] = jnp.zeros((BINS, LANES), jnp.float32)
    idx_copy.wait()
    pl.semaphore_wait(barrier, SHARDS - 1 + len(OFF_PLANE))

    def live_copy(s, src, device):
        return pltpu.make_async_remote_copy(src, lgot.at[s], l_send.at[s], l_recv.at[s], device_id=device)

    live_copies = [live_copy(0, live_v.at[1 - core], partner)]
    live_copies[0].start()

    row_at = lax.broadcasted_iota(jnp.int32, (1, SAMPLES), 1)
    bins = lax.broadcasted_iota(jnp.int32, (BINS, SAMPLES), 0)
    first_row = lax.broadcasted_iota(jnp.int32, (16, SAMPLES), 0) * 60

    def d2d(i):
        part = pl.ds(i * step, step)
        return pltpu.make_async_remote_copy(
            own.at[part], prt.at[part], d2d_send.at[i], d2d_recv.at[i], device_id=partner
        )

    def chunk(i, _):
        in_copy(i).wait()
        for j in range(step):
            b = i * step + j
            before, count = idx_ref[0, b], idx_ref[1, b]
            x = x_buf[b]
            live = row_at < count
            marks = jnp.where(live, marks_ref[pl.ds(b, 1), :], -1)
            hot = jnp.where(bins == marks, 1.0, 0.0).astype(jnp.bfloat16)
            at = jnp.where(live, row_at, -1)
            minute = jnp.where((at >= first_row) & (at < first_row + 60), 1.0, 0.0).astype(jnp.bfloat16)
            both = jnp.dot(jnp.concatenate([hot, minute], axis=0), x, preferred_element_type=jnp.float32)
            own[b] = own[before] + both[:BINS]
            total = both[BINS : BINS + 8]
            high = total.astype(jnp.bfloat16)
            low = (total - high.astype(jnp.float32)).astype(jnp.bfloat16)
            least, most = minute_extremes(x, count)
            st_nat[b] = jnp.concatenate([least, most, high, low], axis=0)
        d2d(i).start()
        return 0

    lax.fori_loop(0, steps, chunk, 0)

    def place(o, _):
        for c in range(CAP):
            st_slots[o, c] = st_nat[idx_ref[2, o * CAP + c]]
        return 0

    lax.fori_loop(0, SHARDS, place, 0)

    def st_copies(d, to, slot):
        device = {"shard": to, "replica": y}
        return [
            pltpu.make_async_remote_copy(
                src.at[to], dst.at[slot], st_send.at[k, d], st_recv.at[k, d], device_id=device
            )
            for k, (src, dst) in enumerate(((st_slots, stats_out), (meta_v, meta_out)))
        ]

    def send_stats(d, _):
        for c in st_copies(d, lax.rem(shard + d, SHARDS), shard):
            c.start()
        return 0

    lax.fori_loop(1, SHARDS, send_stats, 0)
    kept = [
        pltpu.make_async_copy(st_slots.at[shard], stats_out.at[shard], loc_sem.at[0]),
        pltpu.make_async_copy(meta_v.at[shard], meta_out.at[shard], loc_sem.at[1]),
    ]
    for c in kept:
        c.start()

    bases = [[0] * (HALVINGS + 1) for _ in parts]
    copies = [[] for _ in parts]

    def encode(v):
        size = jnp.max(jnp.abs(v), axis=0, keepdims=True)
        gain = jnp.where(size > TINY, LEVELS / jnp.maximum(size, TINY), 0.0)
        code = (v * gain + 32768.5).astype(jnp.int32)
        return (code[:8] << 16) | code[8:], size

    def decode(word, size):
        unit = size * (1.0 / LEVELS)
        high = lax.shift_right_logical(word, 16).astype(jnp.float32)
        low = (word & 0xFFFF).astype(jnp.float32)
        return jnp.concatenate([(high - 32768.0) * unit, (low - 32768.0) * unit], axis=0)

    def each(n, fn):
        unroll = min(n, 8)

        def body(i, _):
            for u in range(unroll):
                fn(i * unroll + u)
            return 0

        lax.fori_loop(0, n // unroll, body, 0)

    def densify(p, lo, to=None):
        rows = pl.ds(p * ROWS, ROWS)

        def one(i):
            e = lo + i
            v = own[idx_ref[8 + p, e], rows] + prt[idx_ref[8 + PARTS + p, e], rows]
            if to is None:
                acc[p][e] = v
            else:
                out[p][to + i], outs[p][to + i] = encode(v)

        each(64, one)

    def add_in(p, at, lo, n, to=None):
        def one(i):
            v = acc[p][at + i] + decode(got[p][lo + i], gots[p][lo + i])
            if to is None:
                acc[p][at + i] = v
            else:
                out[p][to + i], outs[p][to + i] = encode(v)

        each(n, one)

    def offset(s):
        return 128 - (128 >> s)

    def send(p, slot, lo, n, device):
        region = pl.ds(lo, n)
        both = [
            pltpu.make_async_remote_copy(
                src[p].at[region], dst[p].at[region], cube_send.at[k, p, slot], cube_recv.at[k, p, slot], device_id=device,
            )
            for k, (src, dst) in enumerate(((out, got), (outs, gots)))
        ]
        for c in both:
            c.start()
        copies[p].append(both)

    def halve(p, s):
        d = ORDERS[p][s]
        half = 64 >> s
        send(p, s, offset(s), half, across((d,)))
        bases[p][s + 1] = bases[p][s] + bits[d] * half

    for i in range(steps):
        d2d(i).wait_recv()
    for p in parts:
        bit = bits[ORDERS[p][0]]
        densify(p, (1 - bit) * 64, 0)
        halve(p, 0)
        densify(p, bit * 64)

    live_copies[0].wait_recv()
    lbuf[0] = live_v[core] + lgot[0]
    for s in range(1, HALVINGS + 1):
        live_copies.append(live_copy(s, lbuf.at[s - 1], across((ORDERS[0][s - 1],))))
        live_copies[s].start()
        half = 64 >> (s - 1)
        lo = offset(s - 1)
        for p in parts:
            for c in copies[p][s - 1]:
                c.wait_recv()
            base = bases[p][s]
            if s < HALVINGS:
                quarter = half // 2
                bit = bits[ORDERS[p][s]]
                away = (1 - bit) * quarter
                add_in(p, base + away, lo + away, quarter, offset(s))
                halve(p, s)
                add_in(p, base + bit * quarter, lo + bit * quarter, quarter)
            else:
                add_in(p, base, lo, half)
                for m, dims in enumerate(last_groups(p), 1):
                    theirs = base
                    for w, d in zip((half // 2, half // 4, half // 8), ORDERS[p][HALVINGS:]):
                        theirs = theirs + (1 - bits[d] if d in dims else bits[d]) * w
                    spot = offset(HALVINGS) + (m - 1) * 2
                    for k in range(2):
                        out[p][spot + k], outs[p][spot + k] = encode(acc[p][theirs + k])
                    send(p, HALVINGS + m - 1, spot, 2, across(dims))
        live_copies[s].wait_recv()
        lbuf[s] = lbuf[s - 1] + lgot[s]
    for m, dims in enumerate(last_groups(0), 1):
        c = live_copy(HALVINGS + m, lbuf.at[HALVINGS], across(dims))
        c.start()
        live_copies.append(c)
    for p in parts:
        mine = bases[p][HALVINGS]
        for w, d in zip((8, 4, 2), ORDERS[p][HALVINGS:]):
            mine = mine + bits[d] * w
        v = [acc[p][mine + k] for k in range(2)]
        for m in range(1, 8):
            for c in copies[p][HALVINGS + m - 1]:
                c.wait_recv()
            spot = offset(HALVINGS) + (m - 1) * 2
            v = [v[k] + decode(got[p][spot + k], gots[p][spot + k]) for k in range(2)]
        for k in range(2):
            sk_out[k, p * ROWS : (p + 1) * ROWS, :] = v[k]
    total = lbuf[HALVINGS]
    for m in range(1, 8):
        live_copies[HALVINGS + m].wait_recv()
        total = total + lgot[HALVINGS + m]
    live_out[...] = total

    def wait_stats(d, _):
        for c in st_copies(d, shard, lax.rem(shard - d + SHARDS, SHARDS)):
            c.wait_recv()
        return 0

    lax.fori_loop(1, SHARDS, wait_stats, 0)

    def wait_sends(d, _):
        for c in st_copies(d, lax.rem(shard + d, SHARDS), shard):
            c.wait_send()
        return 0

    lax.fori_loop(1, SHARDS, wait_sends, 0)
    for c in kept:
        c.wait()
    for c in live_copies:
        c.wait_send()
    for i in range(steps):
        d2d(i).wait_send()
    for p in parts:
        for both in copies[p]:
            for c in both:
                c.wait_send()


def exchange_call(samples, marks, counts, series, theirs, owner_map):
    step = 8
    vmem = pl.BlockSpec(memory_space=pltpu.VMEM)
    any_ = pl.BlockSpec(memory_space=pl.ANY)
    lane = np.arange(LANES)
    live_at = np.stack([(lane // 8) * 16 + r * 8 + lane % 8 for r in (0, 1)]).astype(np.int32)
    i32, f32, bf16 = jnp.int32, jnp.float32, jnp.bfloat16
    dma = pltpu.SemaphoreType.DMA
    scratch = [
        pltpu.VMEM((BLK, SAMPLES, LANES), bf16),
        pltpu.VMEM((BLK + 1, BINS, LANES), f32),
        pltpu.VMEM((BLK + 1, BINS, LANES), f32),
        pltpu.VMEM((BLK, 32, LANES), bf16),
        pltpu.VMEM((SHARDS, CAP, 32, LANES), bf16),
        pltpu.VMEM((SHARDS, 1, LANES), f32),
        pltpu.VMEM((2, 1, LANES), f32),
        pltpu.VMEM((8 + 2 * PARTS, 128), i32),
        pltpu.SMEM((8 + 2 * PARTS, 128), i32),
        pltpu.VMEM((HALVINGS + 1, 1, LANES), f32),
        pltpu.VMEM((HALVINGS + 8, 1, LANES), f32),
        dma((BLK // step,)),
        dma,
        dma((BLK // step,)),
        dma((BLK // step,)),
        dma((2, PARTS, HALVINGS + 7)),
        dma((2, PARTS, HALVINGS + 7)),
        dma((2, SHARDS)),
        dma((2, SHARDS)),
        dma((HALVINGS + 8,)),
        dma((HALVINGS + 8,)),
        dma((2,)),
    ]
    scratch += [pltpu.VMEM((128, ROWS, LANES), f32)] * PARTS
    scratch += ([pltpu.VMEM((126, 8, LANES), i32)] * PARTS + [pltpu.VMEM((126, 1, LANES), f32)] * PARTS) * 2
    return pl.pallas_call(
        functools.partial(exchange_kernel, step=step),
        in_specs=[any_] + [vmem] * 7,
        out_specs=[vmem, any_, any_, vmem],
        out_shape=[
            jax.ShapeDtypeStruct((2, BINS, LANES), f32),
            jax.ShapeDtypeStruct((SHARDS, CAP, 32, LANES), bf16),
            jax.ShapeDtypeStruct((SHARDS, 1, LANES), f32),
            jax.ShapeDtypeStruct((1, LANES), f32),
        ],
        scratch_shapes=scratch,
        compiler_params=pltpu.CompilerParams(
            collective_id=0, has_side_effects=True, vmem_limit_bytes=60 * 2**20
        ),
        name="exchange",
    )(
        samples, marks, counts.reshape(1, BLK), series.reshape(1, BLK), theirs.reshape(1, BLK),
        owner_map.reshape(1, -1), jnp.asarray(part_positions()), jnp.asarray(live_at),
    )


def finish_kernel(counts, stats, sk_ref, live_ref, cold, sk_out, live_out, st_buf, cold_buf, in_sem, out_sem, *, step):
    steps = SHARDS * CAP // step
    for i in range(steps):
        part = pl.ds(i * step, step)
        pltpu.make_async_copy(stats.at[part], st_buf.at[part], in_sem.at[i]).start()
    minute = lax.broadcasted_iota(jnp.int32, (8, LANES), 0).astype(jnp.float32) * 60.0
    sk_out[...] = sk_ref[...]
    place = lax.div(lax.axis_index("shard"), 2) * 8 + lax.axis_index("replica") * 2
    lane = lax.broadcasted_iota(jnp.int32, (1, LANES), 1)
    for k in range(2):
        live_out[k] = jnp.sum(jnp.where(lane == place + k, live_ref[...], 0.0))
    for i in range(steps):
        part = pl.ds(i * step, step)
        pltpu.make_async_copy(stats.at[part], st_buf.at[part], in_sem.at[i]).wait()

        def group(g, _):
            source = i * (step // CAP) + g
            for c in range(CAP):
                at = source * CAP + c
                count = jnp.clip(counts[source, 0, c] - minute, 0.0, 60.0)
                filled = count > 0
                st = st_buf[at].astype(jnp.float32)
                cold_buf[at, 0] = jnp.where(filled, st[0:8], 0.0)
                cold_buf[at, 1] = jnp.where(filled, st[8:16], 0.0)
                cold_buf[at, 2] = jnp.where(filled, st[16:24] + st[24:32], 0.0)
                cold_buf[at, 3] = count
            return 0

        lax.fori_loop(0, step // CAP, group, 0)
        pltpu.make_async_copy(cold_buf.at[part], cold.at[part], out_sem.at[i]).start()
    for i in range(steps):
        part = pl.ds(i * step, step)
        pltpu.make_async_copy(cold_buf.at[part], cold.at[part], out_sem.at[i]).wait()


def finish_call(counts, stats, sketches, live):
    step = 32
    vmem = pl.BlockSpec(memory_space=pltpu.VMEM)
    smem = pl.BlockSpec(memory_space=pltpu.SMEM)
    any_ = pl.BlockSpec(memory_space=pl.ANY)
    return pl.pallas_call(
        functools.partial(finish_kernel, step=step),
        in_specs=[smem, any_, vmem, vmem],
        out_specs=[any_, vmem, smem],
        out_shape=[
            jax.ShapeDtypeStruct((SHARDS * CAP, 4, 8, LANES), jnp.float32),
            jax.ShapeDtypeStruct((2, BINS, LANES), jnp.float32),
            jax.ShapeDtypeStruct((2,), jnp.float32),
        ],
        scratch_shapes=[
            pltpu.VMEM((SHARDS * CAP, 32, LANES), jnp.bfloat16),
            pltpu.VMEM((SHARDS * CAP, 4, 8, LANES), jnp.float32),
            pltpu.SemaphoreType.DMA((SHARDS * CAP // step,)),
            pltpu.SemaphoreType.DMA((SHARDS * CAP // step,)),
        ],
        name="finish",
    )(counts, stats, sketches, live)


def body(samples, counts, buckets, block_series, owner_map):
    swap = [(i, i ^ 1) for i in range(SHARDS)]
    theirs = lax.ppermute(block_series, "shard", swap)
    sk, st, got_counts, got_live = exchange_call(samples, buckets, counts, block_series, theirs, owner_map)
    cold, sketches, live_rows = finish_call(got_counts, st.reshape(SHARDS * CAP, 32, LANES), sk, got_live)
    return cold.reshape(1, 1, SHARDS * CAP, 4, 8, LANES), sketches, live_rows


def solution(mesh):
    return jax.shard_map(
        body,
        mesh=mesh,
        in_specs=(
            P(("shard", "replica"), None, None),
            P(("shard", "replica")),
            P(("shard", "replica"), None),
            P(("shard", "replica")),
            P(),
        ),
        out_specs=(
            P("shard", "replica", None, None, None, None),
            P(("shard", "replica"), None, None),
            P(("shard", "replica")),
        ),
        check_vma=False,
    )
```

time: 74.2 us -> 66.6 us (0.90)
  Pallas kernels: 71.4 us -> 63.6 us
    pallas_call x2 -> x1, Pallas kernels: 67.4 us -> 59.5 us  [exchange_call(): pl.pallas_call(functools.partial(exchange_kernel, step=step), in_specs=[a...]
where the time goes in v4:
time: 66.6 us; the launch traced here: 66.1 us
  Pallas kernels  63.6 us (95%)
  waiting for transfers between devices  1.28 us (2%)
    pallas_call x1, Pallas kernels, exchange_call(): pl.pallas_call(functools.partial(exchange_kernel, step=step), in_specs=[a...  59.5 us
    pallas_call x1, Pallas kernels, finish_call(): pl.pallas_call(functools.partial(finish_kernel, step=step), in_specs=[sme...  4.02 us
  transfers between devices with their start and end apart: 1, of which 1 were waited for; matrix products, arithmetic and copies ran while one was open for 0% of the time, Pallas kernels for 0%

profile of v4, /device:TPU:0, one launch (start us, length us, event | category | flops | bytes accessed | tf_op | source)
XLA Modules:
  0.0 66.1 jit_solution(16501311992044909766)
XLA Ops:
  0.6 0.1 collective-permute-start
  0.7 1.3 %collective-permute-done = s32[64]{0:T(128)S(1)} collective-permute-done((s32[64]{0:T(128)}, s32[64]{0:T(128)S(1)}, u32[]{:S(2)}, u32[]{:S(2)}) %collective-permute-start) | collective-permute-done | bytes 288 | tf_op jit(solution)/shard_map/ppermute | solution.py:533
  2.0 0.0 copy-start
  2.0 0.5 copy-done
  2.5 59.5 %exchange.1 = (f32[2,128,128]{2,1,0:T(8,128)}, bf16[32,4,32,128]{3,2,1,0:T(8,128)(2,1)}, f32[32,1,128]{2,1,0:T(1,128)}, f32[1,128]{1,0:T(1,128)}) custom-call(bf16[64,480,128]{2,1,0:T(8,128)(2,1)} %samples.1, s32[64,480]{1,0:T(8,128)} %marks_ref.1, s32[1,64]{1,0:T(1,128)} %bitcast.8, s32[1,64]{1,0:T(1,128)} %bitcast.9, s32[1,64]{1,0:T(1,128)} %bitcast.10, ...), custom_call_target="tpu_custom_call" | custom-call | tf_op jit(solution)/shard_map/exchange/pallas_call | solution.py:451
  62.1 4.0 %finish.1 = (f32[128,4,8,128]{3,2,1,0:T(8,128)}, f32[2,128,128]{2,1,0:T(8,128)}, f32[2]{0:T(128)}) custom-call(f32[32,1,128]{2,1,0:T(1,128)} %get-tuple-element.10.counts, bf16[128,32,128]{2,1,0:T(8,128)(2,1)} %bitcast.6, f32[2,128,128]{2,1,0:T(8,128)} %get-tuple-element.12.sk_ref, f32[1,128]{1,0:T(1,128)} %get-tuple-element.13.live_ref), custom_call_target="tpu_custom_call" | custom-call | tf_op jit(solution)/shard_map/finish/pallas_call | solution.py:512
Async XLA Ops:
  0.6 1.4 %collective-permute-start = (s32[64]{0:T(128)}, s32[64]{0:T(128)S(1)}, u32[]{:S(2)}, u32[]{:S(2)}) collective-permute-start(s32[64]{0:T(128)} %param.10), channel_id=1, source_target_pairs={{0,4},{4,0},{8,12},{12,8},{16,20},{20,16},{24,28},{28,24},{32,36},... | collective-permute-start | bytes 776 | tf_op jit(solution)/shard_map/ppermute | solution.py:533
  2.0 0.5 copy-start

commit v5 on v4

v5 whole, which is shorter than its diff:
```python
import functools

import jax
import jax.numpy as jnp
import numpy as np
from jax import lax
from jax.experimental import pallas as pl
from jax.experimental.pallas import tpu as pltpu
from jax.sharding import PartitionSpec as P

BINS = 128
LANES = 128
SAMPLES = 480
BLK = 64
SHARDS = 32
REPLICAS = 4
CAP = 4
DIMS = (("x", 0), ("z", 0), ("y", 0), ("x", 1), ("z", 1), ("y", 1))
GROUPS = (
    ((3, 0, 5), (0, 3, 5)), ((4, 5, 2), (5, 2, 4)), ((1, 0, 3), (0, 3, 1)), ((3, 5, 1), (3, 1, 5)),
    ((2, 0, 4), (4, 2, 0)), ((5, 0, 2), (5, 2, 0)), ((1, 2, 4), (4, 2, 1)), ((2, 5, 4), (5, 2, 4)),
)
EVENTS = (
    (0, 0, 1), (0, 1, 1), (1, 0, 1), (1, 1, 1), (2, 0, 1), (3, 0, 1), (2, 1, 1), (4, 0, 1), (4, 1, 1), (5, 0, 1),
    (0, 0, 2), (6, 0, 1), (3, 1, 1), (2, 0, 2), (7, 0, 1), (6, 1, 1), (5, 1, 1), (0, 1, 2), (1, 1, 2), (4, 0, 2),
    (2, 1, 2), (4, 1, 2), (7, 1, 1), (6, 0, 2), (1, 0, 2), (6, 1, 2), (3, 0, 2), (5, 1, 2), (0, 0, 3), (5, 0, 2),
    (3, 1, 2), (7, 1, 2), (1, 1, 3), (7, 0, 2), (2, 1, 3), (1, 0, 3), (4, 0, 3), (0, 1, 3), (6, 1, 3), (6, 0, 3),
    (5, 0, 3), (3, 0, 3), (2, 0, 3), (4, 1, 3), (3, 1, 3), (7, 1, 3), (5, 1, 3), (7, 0, 3),
)
TAILS = tuple(tuple(d for d in range(6) if d not in g[0]) for g in GROUPS)
PARTS = len(GROUPS)
ROWS = BINS // PARTS
LIMIT = 6.0
LEVELS = 32766.0
TINY = 1e-33
GRAY = {(0, 0): 0, (0, 1): 1, (1, 1): 2, (1, 0): 3}


HALVINGS = 3


def last_groups(p):
    return [tuple(d for k, d in enumerate(TAILS[p]) if m >> k & 1) for m in range(1, 8)]


def off_plane():
    dims = {(d,) for g in GROUPS for d in g[0]}
    dims |= {tuple(sorted(g)) for p in range(PARTS) for g in last_groups(p)}
    return tuple(sorted(g for g in dims if any(DIMS[d][0] == "y" for d in g)))


OFF_PLANE = off_plane()


def part_positions():
    table = np.zeros((PARTS, 128), np.int32)
    for p in range(PARTS):
        for k in range(2):
            order = GROUPS[p][k] + TAILS[p]
            for i in range(64):
                bits = {DIMS[d]: (i >> (5 - s)) & 1 for s, d in enumerate(order)}
                x, y, z = (GRAY[(bits[(a, 1)], bits[(a, 0)])] for a in "xyz")
                table[p, k * 64 + i] = (z * 4 + x) * 16 + y * 2 + k
    return table


def minute_extremes(x, count):
    sub16 = lax.broadcasted_iota(jnp.int16, (16, LANES), 0)
    sub = lax.broadcasted_iota(jnp.int32, (8, LANES), 0)
    least = jnp.zeros((8, LANES), jnp.float32)
    most = jnp.zeros((8, LANES), jnp.float32)
    inf = jnp.bfloat16(jnp.inf)
    for q in range(2):
        lo = [None] * 4
        hi = [None] * 4
        for v in range(15):
            at_row = 240 * q + 16 * v
            val = x[at_row : at_row + 16]
            ok = sub16 < jnp.full((16, LANES), jnp.clip(count - at_row, 0, 16), jnp.int32).astype(jnp.int16)
            small, large = jnp.where(ok, val, inf), jnp.where(ok, val, -inf)
            for h in range(4):
                a, b = 60 * h - 16 * v, 60 * h + 60 - 16 * v
                if b <= 0 or a >= 16:
                    continue
                s, g = small, large
                if a > 0:
                    s, g = jnp.where(sub16 >= a, s, inf), jnp.where(sub16 >= a, g, -inf)
                if b < 16:
                    s, g = jnp.where(sub16 < b, s, inf), jnp.where(sub16 < b, g, -inf)
                lo[h] = s if lo[h] is None else jnp.minimum(lo[h], s)
                hi[h] = g if hi[h] is None else jnp.maximum(hi[h], g)
        for h in range(4):
            m = 4 * q + h
            least = jnp.where(sub == m, jnp.min(lo[h].astype(jnp.float32), axis=0, keepdims=True), least)
            most = jnp.where(sub == m, jnp.max(hi[h].astype(jnp.float32), axis=0, keepdims=True), most)
    return least.astype(jnp.bfloat16), most.astype(jnp.bfloat16)


def iota(shape, dim):
    return lax.broadcasted_iota(jnp.int32, shape, dim)


def routing(series_row, map_row):
    sub, lane = iota((BLK, BLK), 0), iota((BLK, BLK), 1)
    eye = sub == lane

    def row(col):
        return jnp.sum(jnp.where(eye, col, 0), axis=0, keepdims=True)

    series = jnp.sum(jnp.where(eye, series_row, 0), axis=1, keepdims=True)
    pos = jnp.sum(jnp.where(iota((BLK, 256), 1) == series, map_row, 0), axis=1, keepdims=True)
    pos_r = row(pos)
    owner, owner_r = pos >> 3, pos_r >> 3
    rank = jnp.sum(jnp.where((owner == owner_r) & (lane < sub), 1, 0), axis=1, keepdims=True)
    return pos, owner, rank, pos_r, owner_r


def flip(v, bit):
    return v + 1 - 2 * lax.rem(v, 2) if bit == 0 else 3 - v


def exchange_kernel(
    samples, marks_ref, counts_ref, series_ref, theirs_ref, map_ref, target_ref, live_at,
    sk_out, ends_out, sums_out, meta_out, live_out,
    x_buf, own, ends_nat, ends_slots, sums_nat, sums_slots, meta_v, live_v, idx_v, idx_ref, lbuf, lgot,
    in_sem, idx_sem, d2d_send, d2d_recv, cube_send, cube_recv, st_send, st_recv, l_send, l_recv, loc_sem,
    *rest, step,
):
    acc, prt, out, outs, got, gots = (rest[PARTS * i : PARTS * (i + 1)] for i in range(6))
    steps = BLK // step
    parts = tuple(range(PARTS))

    def in_copy(i):
        part = pl.ds(i * step, step)
        return pltpu.make_async_copy(samples.at[part], x_buf.at[part], in_sem.at[i])

    for i in range(steps):
        in_copy(i).start()

    shard = lax.axis_index("shard")
    y = lax.axis_index("replica")
    core = lax.rem(shard, 2)
    x = lax.rem(lax.div(shard, 2), 4)
    z = lax.div(shard, 8)

    def across(dims):
        v = {"x": x, "y": y, "z": z}
        for d in dims:
            axis, bit = DIMS[d]
            v[axis] = flip(v[axis], bit)
        return {"shard": v["z"] * 8 + v["x"] * 2 + core, "replica": v["y"]}

    def bit_of(d):
        axis, bit = DIMS[d]
        v = {"x": x, "y": y, "z": z}[axis]
        high = lax.div(v, 2)
        return high if bit == 1 else lax.rem(v + high, 2)

    bits = [bit_of(d) for d in range(6)]
    partner = {"shard": shard + 1 - 2 * core, "replica": y}

    barrier = pltpu.get_barrier_semaphore()

    def greet(d, _):
        pl.semaphore_signal(barrier, inc=1, device_id={"shard": lax.rem(shard + d, SHARDS), "replica": y})
        return 0

    lax.fori_loop(1, SHARDS, greet, 0)
    for dims in OFF_PLANE:
        pl.semaphore_signal(barrier, inc=1, device_id=across(dims))

    map_row = map_ref[...]
    pos, owner, rank, pos_r, owner_r = routing(series_ref[...], map_row)
    sub, lane = iota((BLK, BLK), 0), iota((BLK, BLK), 1)
    before = jnp.max(jnp.where((pos == pos_r) & (sub < lane), sub, -1), axis=0, keepdims=True)
    idx_v[0:1, 0:BLK] = jnp.where(before < 0, BLK, jnp.minimum(before, BLK))
    idx_v[1:2, 0:BLK] = counts_ref[...]
    block = iota((BLK, LANES), 0)
    filled = iota((BLK, LANES), 1) == owner * CAP + rank
    idx_v[2:3, :] = jnp.clip(jnp.max(jnp.where(filled, block, 0), axis=0, keepdims=True), 0, BLK - 1)
    their_pos = routing(theirs_ref[...], map_row)[0]
    for p in parts:
        want = target_ref[p : p + 1, :] + core * 8
        for k, at in enumerate((pos, their_pos)):
            hit = jnp.max(jnp.where(at == want, block, -1), axis=0, keepdims=True)
            row = 8 + k * PARTS + p
            idx_v[row : row + 1, :] = jnp.where(hit < 0, BLK, jnp.minimum(hit, BLK))
    idx_copy = pltpu.make_async_copy(idx_v, idx_ref, idx_sem)
    idx_copy.start()
    counts_row = counts_ref[...].astype(jnp.float32)
    counts_col = jnp.sum(jnp.where(sub == lane, counts_row, 0.0), axis=1, keepdims=True)
    for r in range(2):
        at = live_at[r : r + 1, :]
        live_v[r] = jnp.sum(jnp.where(pos == at, counts_col, 0.0), axis=0, keepdims=True)
    pick = jnp.where(iota((SHARDS, BLK), 0) == owner_r, 1.0, 0.0)
    put = jnp.where(iota((BLK, LANES), 1) == rank, counts_col, 0.0)
    meta = jnp.dot(pick, put, precision=lax.Precision.HIGHEST, preferred_element_type=jnp.float32)
    for o in range(SHARDS):
        meta_v[o] = meta[o : o + 1, :]
    own[BLK] = jnp.zeros((BINS, LANES), jnp.float32)
    for p in parts:
        prt[p][BLK] = jnp.zeros((ROWS, LANES), jnp.float32)
    idx_copy.wait()

    row_at = lax.broadcasted_iota(jnp.int32, (1, SAMPLES), 1)
    bins = lax.broadcasted_iota(jnp.int32, (BINS, SAMPLES), 0)
    first_row = lax.broadcasted_iota(jnp.int32, (16, SAMPLES), 0) * 60

    first_minute = lax.broadcasted_iota(jnp.int32, (8, LANES), 0) * 60

    def chunk(i, _):
        in_copy(i).wait()
        for j in range(step):
            b = i * step + j
            before, count = idx_ref[0, b], idx_ref[1, b]
            block = x_buf[b]
            live = row_at < count
            marks = jnp.where(live, marks_ref[pl.ds(b, 1), :], -1)
            hot = jnp.where(bins == marks, 1.0, 0.0).astype(jnp.bfloat16)
            at = jnp.where(live, row_at, -1)
            minute = jnp.where((at >= first_row) & (at < first_row + 60), 1.0, 0.0).astype(jnp.bfloat16)
            both = jnp.dot(jnp.concatenate([hot, minute], axis=0), block, preferred_element_type=jnp.float32)
            own[b] = own[before] + both[:BINS]
            rows = jnp.clip(count - first_minute, 1, 60).astype(jnp.float32)
            code = (both[BINS : BINS + 8] * ((LEVELS / LIMIT) / rows) + 32768.5).astype(jnp.int32)
            sums_nat[b] = (code[:4] << 16) | code[4:]
        return 0

    lax.fori_loop(0, steps, chunk, 0)
    pl.semaphore_wait(barrier, SHARDS - 1 + len(OFF_PLANE))

    def d2d(p):
        return pltpu.make_async_remote_copy(
            own.at[pl.ds(0, BLK), pl.ds(p * ROWS, ROWS)], prt[p].at[pl.ds(0, BLK)],
            d2d_send.at[p], d2d_recv.at[p], device_id=partner,
        )

    for p in parts:
        d2d(p).start()

    def live_copy(s, src, device):
        return pltpu.make_async_remote_copy(src, lgot.at[s], l_send.at[s], l_recv.at[s], device_id=device)

    live_copies = [live_copy(0, live_v.at[1 - core], partner)]
    live_copies[0].start()

    def ends(i, _):
        for j in range(4):
            b = i * 4 + j
            least, most = minute_extremes(x_buf[b], idx_ref[1, b])
            ends_nat[b] = jnp.concatenate([least, most], axis=0)
        return 0

    def st_copies(d, to, slot):
        device = {"shard": to, "replica": y}
        pairs = ((ends_slots, ends_out), (sums_slots, sums_out), (meta_v, meta_out))
        return [
            pltpu.make_async_remote_copy(
                src.at[to], dst.at[slot], st_send.at[k, d], st_recv.at[k, d], device_id=device
            )
            for k, (src, dst) in enumerate(pairs)
        ]

    kept = [
        pltpu.make_async_copy(src.at[shard], dst.at[shard], loc_sem.at[k])
        for k, (src, dst) in enumerate(((ends_slots, ends_out), (sums_slots, sums_out), (meta_v, meta_out)))
    ]

    def send_all_stats():
        def place(o, _):
            for c in range(CAP):
                b = idx_ref[2, o * CAP + c]
                ends_slots[o, c] = ends_nat[b]
                sums_slots[o, c] = sums_nat[b]
            return 0

        lax.fori_loop(0, SHARDS, place, 0)

        def send_stats(d, _):
            for c in st_copies(d, lax.rem(shard + d, SHARDS), shard):
                c.start()
            return 0

        lax.fori_loop(1, SHARDS, send_stats, 0)
        for c in kept:
            c.start()

    bases = {(p, k): [k * 64] for p in parts for k in range(2)}
    copies = {}

    def encode(v):
        size = jnp.max(jnp.abs(v), axis=0, keepdims=True)
        gain = jnp.where(size > TINY, LEVELS / jnp.maximum(size, TINY), 0.0)
        code = (v * gain + 32768.5).astype(jnp.int32)
        return (code[:8] << 16) | code[8:], size

    def decode(word, size):
        unit = size * (1.0 / LEVELS)
        high = lax.shift_right_logical(word, 16).astype(jnp.float32)
        low = (word & 0xFFFF).astype(jnp.float32)
        return jnp.concatenate([(high - 32768.0) * unit, (low - 32768.0) * unit], axis=0)

    def each(n, fn):
        unroll = min(n, 8)

        def body(i, _):
            for u in range(unroll):
                fn(i * unroll + u)
            return 0

        lax.fori_loop(0, n // unroll, body, 0)

    def densify(p, lo, to=None):
        rows = pl.ds(p * ROWS, ROWS)

        def one(i):
            e = lo + i
            v = own[idx_ref[8 + p, e], rows] + prt[p][idx_ref[8 + PARTS + p, e]]
            if to is None:
                acc[p][e] = v
            else:
                out[p][to + i], outs[p][to + i] = encode(v)

        each(32, one)

    def add_in(p, at, lo, n, to=None):
        def one(i):
            v = acc[p][at + i] + decode(got[p][lo + i], gots[p][lo + i])
            if to is None:
                acc[p][at + i] = v
            else:
                out[p][to + i], outs[p][to + i] = encode(v)

        each(n, one)

    def spot(k, s):
        return k * 56 + 64 - (64 >> s)

    def send(p, slot, lo, n, device):
        region = pl.ds(lo, n)
        both = [
            pltpu.make_async_remote_copy(
                src[p].at[region], dst[p].at[region], cube_send.at[j, p, slot], cube_recv.at[j, p, slot], device_id=device,
            )
            for j, (src, dst) in enumerate(((out, got), (outs, gots)))
        ]
        for c in both:
            c.start()
        copies[p, slot] = both

    def halve(p, k, s):
        d = GROUPS[p][k][s]
        half = 32 >> s
        send(p, k * HALVINGS + s, spot(k, s), half, across((d,)))
        bases[p, k].append(bases[p, k][s] + bits[d] * half)

    for p in parts:
        lax.fori_loop(p * 2, p * 2 + 2, ends, 0)
        d2d(p).wait_recv()
        for k in range(2):
            bit = bits[GROUPS[p][k][0]]
            densify(p, k * 64 + (1 - bit) * 32, spot(k, 0))
            halve(p, k, 0)
            densify(p, k * 64 + bit * 32)
    send_all_stats()

    live_copies[0].wait_recv()
    lbuf[0] = live_v[core] + lgot[0]

    def live_step(s):
        live_copies.append(live_copy(s, lbuf.at[s - 1], across((GROUPS[0][0][s - 1],))))
        live_copies[s].start()

    live_step(1)
    ready = set()
    for p, k, s in EVENTS:
        if (p, k) == (0, 0):
            live_copies[s].wait_recv()
            lbuf[s] = lbuf[s - 1] + lgot[s]
            if s < HALVINGS:
                live_step(s + 1)
            else:
                for m, dims in enumerate(last_groups(0), 1):
                    c = live_copy(HALVINGS + m, lbuf.at[HALVINGS], across(dims))
                    c.start()
                    live_copies.append(c)
        for c in copies[p, k * HALVINGS + s - 1]:
            c.wait_recv()
        base, lo, half = bases[p, k][s], spot(k, s - 1), 32 >> (s - 1)
        if s < HALVINGS:
            quarter = half // 2
            bit = bits[GROUPS[p][k][s]]
            away = (1 - bit) * quarter
            add_in(p, base + away, lo + away, quarter, spot(k, s))
            halve(p, k, s)
            add_in(p, base + bit * quarter, lo + bit * quarter, quarter)
            continue
        add_in(p, base, lo, half)
        ready.add((p, k))
        if (p, 1 - k) not in ready:
            continue
        for m, dims in enumerate(last_groups(p), 1):
            theirs = 0
            for w, d in zip((4, 2, 1), TAILS[p]):
                theirs = theirs + (1 - bits[d] if d in dims else bits[d]) * w
            at = 112 + (m - 1) * 2
            for j in range(2):
                out[p][at + j], outs[p][at + j] = encode(acc[p][bases[p, j][HALVINGS] + theirs])
            send(p, 2 * HALVINGS + m - 1, at, 2, across(dims))
    for p in parts:
        mine = bits[TAILS[p][0]] * 4 + bits[TAILS[p][1]] * 2 + bits[TAILS[p][2]]
        v = [acc[p][bases[p, k][HALVINGS] + mine] for k in range(2)]
        for m in range(1, 8):
            for c in copies[p, 2 * HALVINGS + m - 1]:
                c.wait_recv()
            at = 112 + (m - 1) * 2
            v = [v[k] + decode(got[p][at + k], gots[p][at + k]) for k in range(2)]
        for k in range(2):
            sk_out[k, p * ROWS : (p + 1) * ROWS, :] = v[k]
    total = lbuf[HALVINGS]
    for m in range(1, 8):
        live_copies[HALVINGS + m].wait_recv()
        total = total + lgot[HALVINGS + m]
    live_out[...] = total

    def wait_stats(d, _):
        for c in st_copies(d, shard, lax.rem(shard - d + SHARDS, SHARDS)):
            c.wait_recv()
        return 0

    lax.fori_loop(1, SHARDS, wait_stats, 0)

    def wait_sends(d, _):
        for c in st_copies(d, lax.rem(shard + d, SHARDS), shard):
            c.wait_send()
        return 0

    lax.fori_loop(1, SHARDS, wait_sends, 0)
    for c in kept:
        c.wait()
    for c in live_copies:
        c.wait_send()
    for p in parts:
        d2d(p).wait_send()
    for both in copies.values():
        for c in both:
            c.wait_send()


def exchange_call(samples, marks, counts, series, theirs, owner_map):
    step = 8
    vmem = pl.BlockSpec(memory_space=pltpu.VMEM)
    any_ = pl.BlockSpec(memory_space=pl.ANY)
    lane = np.arange(LANES)
    live_at = np.stack([(lane // 8) * 16 + r * 8 + lane % 8 for r in (0, 1)]).astype(np.int32)
    i32, f32, bf16 = jnp.int32, jnp.float32, jnp.bfloat16
    dma = pltpu.SemaphoreType.DMA
    scratch = [
        pltpu.VMEM((BLK, SAMPLES, LANES), bf16),
        pltpu.VMEM((BLK + 1, BINS, LANES), f32),
        pltpu.VMEM((BLK, 16, LANES), bf16),
        pltpu.VMEM((SHARDS, CAP, 16, LANES), bf16),
        pltpu.VMEM((BLK, 4, LANES), i32),
        pltpu.VMEM((SHARDS, CAP, 4, LANES), i32),
        pltpu.VMEM((SHARDS, 1, LANES), f32),
        pltpu.VMEM((2, 1, LANES), f32),
        pltpu.VMEM((8 + 2 * PARTS, 128), i32),
        pltpu.SMEM((8 + 2 * PARTS, 128), i32),
        pltpu.VMEM((HALVINGS + 1, 1, LANES), f32),
        pltpu.VMEM((HALVINGS + 8, 1, LANES), f32),
        dma((BLK // step,)),
        dma,
        dma((PARTS,)),
        dma((PARTS,)),
        dma((2, PARTS, 2 * HALVINGS + 7)),
        dma((2, PARTS, 2 * HALVINGS + 7)),
        dma((3, SHARDS)),
        dma((3, SHARDS)),
        dma((HALVINGS + 8,)),
        dma((HALVINGS + 8,)),
        dma((3,)),
    ]
    scratch += [pltpu.VMEM((128, ROWS, LANES), f32)] * PARTS + [pltpu.VMEM((BLK + 1, ROWS, LANES), f32)] * PARTS
    scratch += ([pltpu.VMEM((126, 8, LANES), i32)] * PARTS + [pltpu.VMEM((126, 1, LANES), f32)] * PARTS) * 2
    return pl.pallas_call(
        functools.partial(exchange_kernel, step=step),
        in_specs=[any_] + [vmem] * 7,
        out_specs=[vmem, any_, any_, any_, vmem],
        out_shape=[
            jax.ShapeDtypeStruct((2, BINS, LANES), f32),
            jax.ShapeDtypeStruct((SHARDS, CAP, 16, LANES), bf16),
            jax.ShapeDtypeStruct((SHARDS, CAP, 4, LANES), i32),
            jax.ShapeDtypeStruct((SHARDS, 1, LANES), f32),
            jax.ShapeDtypeStruct((1, LANES), f32),
        ],
        scratch_shapes=scratch,
        compiler_params=pltpu.CompilerParams(
            collective_id=0, has_side_effects=True, vmem_limit_bytes=60 * 2**20
        ),
        name="exchange",
    )(
        samples, marks, counts.reshape(1, BLK), series.reshape(1, BLK), theirs.reshape(1, BLK),
        owner_map.reshape(1, -1), jnp.asarray(part_positions()), jnp.asarray(live_at),
    )


def finish_kernel(
    meta, ends, sums, sk_in, live_in, cold, sk_out, live_out,
    counts, ends_buf, sums_buf, cold_buf, sk_buf, live_buf, in_sem, out_sem, one_sem, *, step,
):
    steps = SHARDS // step

    def loads(i):
        part = pl.ds(i * step, step)
        return [
            pltpu.make_async_copy(src.at[part], dst.at[part], in_sem.at[k, i])
            for k, (src, dst) in enumerate(((ends, ends_buf), (sums, sums_buf)))
        ]

    def store(i):
        part = pl.ds(i * step * CAP, step * CAP)
        return pltpu.make_async_copy(cold_buf.at[part], cold.at[part], out_sem.at[i])

    singles = [
        pltpu.make_async_copy(src, dst, one_sem.at[k])
        for k, (src, dst) in enumerate(((meta, counts), (sk_in, sk_buf), (live_in, live_buf), (sk_buf, sk_out)))
    ]
    singles[0].start()
    for i in range(steps):
        for c in loads(i):
            c.start()
    singles[1].start()
    singles[2].start()
    minute = lax.broadcasted_iota(jnp.int32, (8, LANES), 0).astype(jnp.float32) * 60.0
    singles[0].wait()
    for i in range(steps):
        for c in loads(i):
            c.wait()

        def group(g, _):
            source = i * step + g
            for c in range(CAP):
                at = source * CAP + c
                count = jnp.clip(counts[source, 0, c] - minute, 0.0, 60.0)
                filled = count > 0
                low_high = ends_buf[source, c].astype(jnp.float32)
                word = sums_buf[source, c]
                code = jnp.concatenate([lax.shift_right_logical(word, 16), word & 0xFFFF], axis=0)
                total = (code.astype(jnp.float32) - 32768.0) * (count * (LIMIT / LEVELS))
                cold_buf[at, 0] = jnp.where(filled, low_high[0:8], 0.0)
                cold_buf[at, 1] = jnp.where(filled, low_high[8:16], 0.0)
                cold_buf[at, 2] = jnp.where(filled, total, 0.0)
                cold_buf[at, 3] = count
            return 0

        lax.fori_loop(0, step, group, 0)
        store(i).start()
    singles[1].wait()
    singles[3].start()
    singles[2].wait()
    place = lax.div(lax.axis_index("shard"), 2) * 8 + lax.axis_index("replica") * 2
    lane = lax.broadcasted_iota(jnp.int32, (1, LANES), 1)
    for k in range(2):
        live_out[k] = jnp.sum(jnp.where(lane == place + k, live_buf[...], 0.0))
    singles[3].wait()
    for i in range(steps):
        store(i).wait()


def finish_call(meta, ends, sums, sketches, live):
    step = 8
    smem = pl.BlockSpec(memory_space=pltpu.SMEM)
    any_ = pl.BlockSpec(memory_space=pl.ANY)
    f32 = jnp.float32
    return pl.pallas_call(
        functools.partial(finish_kernel, step=step),
        in_specs=[any_] * 5,
        out_specs=[any_, any_, smem],
        out_shape=[
            jax.ShapeDtypeStruct((SHARDS * CAP, 4, 8, LANES), f32),
            jax.ShapeDtypeStruct((2, BINS, LANES), f32),
            jax.ShapeDtypeStruct((2,), f32),
        ],
        scratch_shapes=[
            pltpu.SMEM((SHARDS, 1, LANES), f32),
            pltpu.VMEM((SHARDS, CAP, 16, LANES), jnp.bfloat16),
            pltpu.VMEM((SHARDS, CAP, 4, LANES), jnp.int32),
            pltpu.VMEM((SHARDS * CAP, 4, 8, LANES), f32),
            pltpu.VMEM((2, BINS, LANES), f32),
            pltpu.VMEM((1, LANES), f32),
            pltpu.SemaphoreType.DMA((2, SHARDS // step)),
            pltpu.SemaphoreType.DMA((SHARDS // step,)),
            pltpu.SemaphoreType.DMA((4,)),
        ],
        name="finish",
    )(meta, ends, sums, sketches, live)


def body(samples, counts, buckets, block_series, owner_map):
    swap = [(i, i ^ 1) for i in range(SHARDS)]
    theirs = lax.ppermute(block_series, "shard", swap)
    sk, ends, sums, meta, live = exchange_call(samples, buckets, counts, block_series, theirs, owner_map)
    cold, sketches, live_rows = finish_call(meta, ends, sums, sk, live)
    return cold.reshape(1, 1, SHARDS * CAP, 4, 8, LANES), sketches, live_rows


def solution(mesh):
    return jax.shard_map(
        body,
        mesh=mesh,
        in_specs=(
            P(("shard", "replica"), None, None),
            P(("shard", "replica")),
            P(("shard", "replica"), None),
            P(("shard", "replica")),
            P(),
        ),
        out_specs=(
            P("shard", "replica", None, None, None, None),
            P(("shard", "replica"), None, None),
            P(("shard", "replica")),
        ),
        check_vma=False,
    )
```

time: 66.6 us -> 68.5 us (1.029)
  Pallas kernels: 63.6 us -> 65.8 us
    pallas_call x1, Pallas kernels: 59.5 us -> 62.6 us  [exchange_call(): pl.pallas_call(functools.partial(exchange_kernel, step=step), in_specs=[a...]
    pallas_call x1, Pallas kernels: 4.02 us -> 3.19 us  [finish_call(): pl.pallas_call(functools.partial(finish_kernel, step=step), in_specs=[any...]
where the time goes in v5:
time: 68.5 us; the launch traced here: 68.3 us
  Pallas kernels  65.8 us (96%)
  waiting for transfers between devices  1.28 us (2%)
    pallas_call x1, Pallas kernels, exchange_call(): pl.pallas_call(functools.partial(exchange_kernel, step=step), in_specs=[a...  62.6 us
    pallas_call x1, Pallas kernels, finish_call(): pl.pallas_call(functools.partial(finish_kernel, step=step), in_specs=[any...  3.19 us
  transfers between devices with their start and end apart: 1, of which 1 were waited for; matrix products, arithmetic and copies ran while one was open for 0% of the time, Pallas kernels for 0%

profile of v5, /device:TPU:0, one launch (start us, length us, event | category | flops | bytes accessed | tf_op | source)
XLA Modules:
  0.0 68.3 jit_solution(16621660399790328595)
XLA Ops:
  0.6 0.1 collective-permute-start
  0.7 1.3 %collective-permute-done = s32[64]{0:T(128)S(1)} collective-permute-done((s32[64]{0:T(128)}, s32[64]{0:T(128)S(1)}, u32[]{:S(2)}, u32[]{:S(2)}) %collective-permute-start) | collective-permute-done | bytes 288 | tf_op jit(solution)/shard_map/ppermute | solution.py:601
  2.0 0.0 copy-start
  2.0 0.5 copy-done
  2.5 62.6 %exchange.1 = (f32[2,128,128]{2,1,0:T(8,128)}, bf16[32,4,16,128]{3,2,1,0:T(8,128)(2,1)}, s32[32,4,4,128]{3,2,1,0:T(4,128)}, f32[32,1,128]{2,1,0:T(1,128)}, f32[1,128]{1,0:T(1,128)}) custom-call(bf16[64,480,128]{2,1,0:T(8,128)(2,1)} %samples.1, s32[64,480]{1,0:T(8,128)} %marks_ref.1, s32[1,64]{1,0:T(1,128)} %bitcast.6, s32[1,64]{1,0:T(1,128)} %bitcast.7, ...), custom_call_target="tpu_custom_call" | custom-call | tf_op jit(solution)/shard_map/exchange/pallas_call | solution.py:485
  65.1 3.2 %finish.1 = (f32[128,4,8,128]{3,2,1,0:T(8,128)}, f32[2,128,128]{2,1,0:T(8,128)}, f32[2]{0:T(128)}) custom-call(f32[32,1,128]{2,1,0:T(1,128)} %get-tuple-element.11.meta, bf16[32,4,16,128]{3,2,1,0:T(8,128)(2,1)} %get-tuple-element.12.ends, s32[32,4,4,128]{3,2,1,0:T(4,128)} %get-tuple-element.13.sums, f32[2,128,128]{2,1,0:T(8,128)} %get-tuple-element.14.sk_in, ...), custom_call_target="tpu_custom_call" | custom-call | tf_op jit(solution)/shard_map/finish/pallas_call | solution.py:575
Async XLA Ops:
  0.6 1.4 %collective-permute-start = (s32[64]{0:T(128)}, s32[64]{0:T(128)S(1)}, u32[]{:S(2)}, u32[]{:S(2)}) collective-permute-start(s32[64]{0:T(128)} %param.10), channel_id=1, source_target_pairs={{0,4},{4,0},{8,12},{12,8},{16,20},{20,16},{24,28},{28,24},{32,36},... | collective-permute-start | bytes 776 | tf_op jit(solution)/shard_map/ppermute | solution.py:601
  2.0 0.5 copy-start

commit v6 on v5

--- a/solution.py
+++ b/solution.py
@@ -16,17 +16,8 @@
 REPLICAS = 4
 CAP = 4
 DIMS = (("x", 0), ("z", 0), ("y", 0), ("x", 1), ("z", 1), ("y", 1))
-GROUPS = (
-    ((3, 0, 5), (0, 3, 5)), ((4, 5, 2), (5, 2, 4)), ((1, 0, 3), (0, 3, 1)), ((3, 5, 1), (3, 1, 5)),
-    ((2, 0, 4), (4, 2, 0)), ((5, 0, 2), (5, 2, 0)), ((1, 2, 4), (4, 2, 1)), ((2, 5, 4), (5, 2, 4)),
-)
-EVENTS = (
-    (0, 0, 1), (0, 1, 1), (1, 0, 1), (1, 1, 1), (2, 0, 1), (3, 0, 1), (2, 1, 1), (4, 0, 1), (4, 1, 1), (5, 0, 1),
-    (0, 0, 2), (6, 0, 1), (3, 1, 1), (2, 0, 2), (7, 0, 1), (6, 1, 1), (5, 1, 1), (0, 1, 2), (1, 1, 2), (4, 0, 2),
-    (2, 1, 2), (4, 1, 2), (7, 1, 1), (6, 0, 2), (1, 0, 2), (6, 1, 2), (3, 0, 2), (5, 1, 2), (0, 0, 3), (5, 0, 2),
-    (3, 1, 2), (7, 1, 2), (1, 1, 3), (7, 0, 2), (2, 1, 3), (1, 0, 3), (4, 0, 3), (0, 1, 3), (6, 1, 3), (6, 0, 3),
-    (5, 0, 3), (3, 0, 3), (2, 0, 3), (4, 1, 3), (3, 1, 3), (7, 1, 3), (5, 1, 3), (7, 0, 3),
-)
+GROUPS = (((4, 5, 1), (1, 5, 4)), ((5, 2, 3), (2, 5, 3)), ((3, 2, 5), (5, 3, 2)), ((2, 4, 0), (4, 0, 2)), ((0, 2, 5), (0, 5, 2)), ((5, 1, 2), (2, 5, 1)), ((1, 3, 2), (3, 2, 1)), ((2, 5, 4), (4, 5, 2)))
+EVENTS = ((0, 0, 1), (0, 1, 1), (1, 0, 1), (1, 1, 1), (2, 0, 1), (4, 0, 1), (3, 1, 1), (2, 1, 1), (3, 0, 1), (6, 0, 1), (6, 1, 1), (4, 1, 1), (7, 1, 1), (5, 0, 1), (5, 1, 1), (0, 0, 2), (2, 1, 2), (3, 1, 2), (0, 1, 2), (7, 0, 1), (6, 0, 2), (3, 0, 2), (5, 0, 2), (1, 1, 2), (1, 0, 2), (4, 1, 2), (0, 0, 3), (2, 0, 2), (7, 1, 2), (4, 0, 2), (5, 1, 2), (6, 1, 2), (0, 1, 3), (3, 0, 3), (2, 1, 3), (7, 0, 2), (1, 1, 3), (3, 1, 3), (2, 0, 3), (6, 0, 3), (1, 0, 3), (4, 0, 3), (5, 0, 3), (5, 1, 3), (4, 1, 3), (6, 1, 3), (7, 1, 3), (7, 0, 3))
 TAILS = tuple(tuple(d for d in range(6) if d not in g[0]) for g in GROUPS)
 PARTS = len(GROUPS)
 ROWS = BINS // PARTS
@@ -50,6 +41,7 @@
 
 
 OFF_PLANE = off_plane()
+STATS_ORDER = tuple(sorted(range(1, SHARDS), key=lambda d: (-min((d // 8) % 4, 4 - (d // 8) % 4), -min((d // 2) % 4, 4 - (d // 2) % 4), d)))
 
 
 def part_positions():
@@ -120,10 +112,10 @@
 
 
 def exchange_kernel(
-    samples, marks_ref, counts_ref, series_ref, theirs_ref, map_ref, target_ref, live_at,
+    samples, marks_ref, counts_ref, series_ref, map_ref, target_ref, live_at,
     sk_out, ends_out, sums_out, meta_out, live_out,
-    x_buf, own, ends_nat, ends_slots, sums_nat, sums_slots, meta_v, live_v, idx_v, idx_ref, lbuf, lgot,
-    in_sem, idx_sem, d2d_send, d2d_recv, cube_send, cube_recv, st_send, st_recv, l_send, l_recv, loc_sem,
+    x_buf, own, ends_nat, ends_slots, sums_nat, sums_slots, meta_v, live_v, idx_v, idx_ref, their_series, their_v, their_idx, lbuf, lgot,
+    in_sem, idx_sem, series_sem, d2d_send, d2d_recv, cube_send, cube_recv, st_send, st_recv, l_send, l_recv, loc_sem,
     *rest, step,
 ):
     acc, prt, out, outs, got, gots = (rest[PARTS * i : PARTS * (i + 1)] for i in range(6))
@@ -178,14 +170,14 @@
     block = iota((BLK, LANES), 0)
     filled = iota((BLK, LANES), 1) == owner * CAP + rank
     idx_v[2:3, :] = jnp.clip(jnp.max(jnp.where(filled, block, 0), axis=0, keepdims=True), 0, BLK - 1)
-    their_pos = routing(theirs_ref[...], map_row)[0]
-    for p in parts:
-        want = target_ref[p : p + 1, :] + core * 8
-        for k, at in enumerate((pos, their_pos)):
-            hit = jnp.max(jnp.where(at == want, block, -1), axis=0, keepdims=True)
-            row = 8 + k * PARTS + p
-            idx_v[row : row + 1, :] = jnp.where(hit < 0, BLK, jnp.minimum(hit, BLK))
-    idx_copy = pltpu.make_async_copy(idx_v, idx_ref, idx_sem)
+
+    def last_blocks(at, to, first):
+        for p in parts:
+            hit = jnp.max(jnp.where(at == target_ref[p : p + 1, :] + core * 8, block, -1), axis=0, keepdims=True)
+            to[first + p : first + p + 1, :] = jnp.where(hit < 0, BLK, jnp.minimum(hit, BLK))
+
+    last_blocks(pos, idx_v, 8)
+    idx_copy = pltpu.make_async_copy(idx_v, idx_ref, idx_sem.at[0])
     idx_copy.start()
     counts_row = counts_ref[...].astype(jnp.float32)
     counts_col = jnp.sum(jnp.where(sub == lane, counts_row, 0.0), axis=1, keepdims=True)
@@ -235,7 +227,11 @@
             d2d_send.at[p], d2d_recv.at[p], device_id=partner,
         )
 
-    for p in parts:
+    series_copy = pltpu.make_async_remote_copy(
+        series_ref, their_series, series_sem.at[0], series_sem.at[1], device_id=partner
+    )
+    series_copy.start()
+    for p in parts[:4]:
         d2d(p).start()
 
     def live_copy(s, src, device):
@@ -266,24 +262,20 @@
         for k, (src, dst) in enumerate(((ends_slots, ends_out), (sums_slots, sums_out), (meta_v, meta_out)))
     ]
 
-    def send_all_stats():
-        def place(o, _):
-            for c in range(CAP):
-                b = idx_ref[2, o * CAP + c]
-                ends_slots[o, c] = ends_nat[b]
-                sums_slots[o, c] = sums_nat[b]
-            return 0
-
-        lax.fori_loop(0, SHARDS, place, 0)
-
-        def send_stats(d, _):
+    def place(o, _):
+        for c in range(CAP):
+            b = idx_ref[2, o * CAP + c]
+            ends_slots[o, c] = ends_nat[b]
+            sums_slots[o, c] = sums_nat[b]
+        return 0
+
+    peers = iter(STATS_ORDER)
+
+    def next_stats():
+        d = next(peers, None)
+        if d is not None:
             for c in st_copies(d, lax.rem(shard + d, SHARDS), shard):
                 c.start()
-            return 0
-
-        lax.fori_loop(1, SHARDS, send_stats, 0)
-        for c in kept:
-            c.start()
 
     bases = {(p, k): [k * 64] for p in parts for k in range(2)}
     copies = {}
@@ -315,7 +307,7 @@
 
         def one(i):
             e = lo + i
-            v = own[idx_ref[8 + p, e], rows] + prt[p][idx_ref[8 + PARTS + p, e]]
+            v = own[idx_ref[8 + p, e], rows] + prt[p][their_idx[p, e]]
             if to is None:
                 acc[p][e] = v
             else:
@@ -354,16 +346,27 @@
         send(p, k * HALVINGS + s, spot(k, s), half, across((d,)))
         bases[p, k].append(bases[p, k][s] + bits[d] * half)
 
+    lax.fori_loop(0, 3, ends, 0)
+    series_copy.wait_recv()
+    last_blocks(routing(their_series[...], map_row)[0], their_v, 0)
+    their_copy = pltpu.make_async_copy(their_v, their_idx, idx_sem.at[1])
+    their_copy.start()
+    lax.fori_loop(3, 7, ends, 0)
+    their_copy.wait()
     for p in parts:
-        lax.fori_loop(p * 2, p * 2 + 2, ends, 0)
         d2d(p).wait_recv()
+        if p + 4 < PARTS:
+            d2d(p + 4).start()
         for k in range(2):
             bit = bits[GROUPS[p][k][0]]
             densify(p, k * 64 + (1 - bit) * 32, spot(k, 0))
             halve(p, k, 0)
             densify(p, k * 64 + bit * 32)
-    send_all_stats()
-
+
+    lax.fori_loop(7, BLK // 4, ends, 0)
+    lax.fori_loop(0, SHARDS, place, 0)
+    for c in kept:
+        c.start()
     live_copies[0].wait_recv()
     lbuf[0] = live_v[core] + lgot[0]
 
@@ -386,6 +389,7 @@
                     live_copies.append(c)
         for c in copies[p, k * HALVINGS + s - 1]:
             c.wait_recv()
+        next_stats()
         base, lo, half = bases[p, k][s], spot(k, s - 1), 32 >> (s - 1)
         if s < HALVINGS:
             quarter = half // 2
@@ -399,14 +403,33 @@
         ready.add((p, k))
         if (p, 1 - k) not in ready:
             continue
-        for m, dims in enumerate(last_groups(p), 1):
+        values = []
+        for dims in last_groups(p):
             theirs = 0
             for w, d in zip((4, 2, 1), TAILS[p]):
                 theirs = theirs + (1 - bits[d] if d in dims else bits[d]) * w
-            at = 112 + (m - 1) * 2
-            for j in range(2):
-                out[p][at + j], outs[p][at + j] = encode(acc[p][bases[p, j][HALVINGS] + theirs])
-            send(p, 2 * HALVINGS + m - 1, at, 2, across(dims))
+            values += [acc[p][bases[p, j][HALVINGS] + theirs] for j in range(2)]
+        for i, (word, size) in enumerate([encode(v) for v in values]):
+            out[p][112 + i], outs[p][112 + i] = word, size
+        for m, dims in enumerate(last_groups(p), 1):
+            send(p, 2 * HALVINGS + m - 1, 112 + (m - 1) * 2, 2, across(dims))
+    def wait_stats(d, _):
+        for c in st_copies(d, shard, lax.rem(shard - d + SHARDS, SHARDS)):
+            c.wait_recv()
+        for c in st_copies(d, lax.rem(shard + d, SHARDS), shard):
+            c.wait_send()
+        return 0
+
+    for p in parts:
+        d2d(p).wait_send()
+        for slot in range(2 * HALVINGS):
+            for c in copies[p, slot]:
+                c.wait_send()
+    series_copy.wait_send()
+    lax.fori_loop(1, SHARDS, wait_stats, 0)
+    for c in kept:
+        c.wait()
+
     for p in parts:
         mine = bits[TAILS[p][0]] * 4 + bits[TAILS[p][1]] * 2 + bits[TAILS[p][2]]
         v = [acc[p][bases[p, k][HALVINGS] + mine] for k in range(2)]
@@ -423,31 +446,15 @@
         total = total + lgot[HALVINGS + m]
     live_out[...] = total
 
-    def wait_stats(d, _):
-        for c in st_copies(d, shard, lax.rem(shard - d + SHARDS, SHARDS)):
-            c.wait_recv()
-        return 0
-
-    lax.fori_loop(1, SHARDS, wait_stats, 0)
-
-    def wait_sends(d, _):
-        for c in st_copies(d, lax.rem(shard + d, SHARDS), shard):
-            c.wait_send()
-        return 0
-
-    lax.fori_loop(1, SHARDS, wait_sends, 0)
-    for c in kept:
-        c.wait()
     for c in live_copies:
         c.wait_send()
     for p in parts:
-        d2d(p).wait_send()
-    for both in copies.values():
-        for c in both:
-            c.wait_send()
-
-
-def exchange_call(samples, marks, counts, series, theirs, owner_map):
+        for slot in range(2 * HALVINGS, 2 * HALVINGS + 7):
+            for c in copies[p, slot]:
+                c.wait_send()
+
+
+def exchange_call(samples, marks, counts, series, owner_map):
     step = 8
     vmem = pl.BlockSpec(memory_space=pltpu.VMEM)
     any_ = pl.BlockSpec(memory_space=pl.ANY)
@@ -464,12 +471,16 @@
         pltpu.VMEM((SHARDS, CAP, 4, LANES), i32),
         pltpu.VMEM((SHARDS, 1, LANES), f32),
         pltpu.VMEM((2, 1, LANES), f32),
-        pltpu.VMEM((8 + 2 * PARTS, 128), i32),
-        pltpu.SMEM((8 + 2 * PARTS, 128), i32),
+        pltpu.VMEM((8 + PARTS, 128), i32),
+        pltpu.SMEM((8 + PARTS, 128), i32),
+        pltpu.VMEM((1, BLK), i32),
+        pltpu.VMEM((PARTS, 128), i32),
+        pltpu.SMEM((PARTS, 128), i32),
         pltpu.VMEM((HALVINGS + 1, 1, LANES), f32),
         pltpu.VMEM((HALVINGS + 8, 1, LANES), f32),
         dma((BLK // step,)),
-        dma,
+        dma((2,)),
+        dma((2,)),
         dma((PARTS,)),
         dma((PARTS,)),
         dma((2, PARTS, 2 * HALVINGS + 7)),
@@ -484,7 +495,7 @@
     scratch += ([pltpu.VMEM((126, 8, LANES), i32)] * PARTS + [pltpu.VMEM((126, 1, LANES), f32)] * PARTS) * 2
     return pl.pallas_call(
         functools.partial(exchange_kernel, step=step),
-        in_specs=[any_] + [vmem] * 7,
+        in_specs=[any_] + [vmem] * 6,
         out_specs=[vmem, any_, any_, any_, vmem],
         out_shape=[
             jax.ShapeDtypeStruct((2, BINS, LANES), f32),
@@ -499,8 +510,8 @@
         ),
         name="exchange",
     )(
-        samples, marks, counts.reshape(1, BLK), series.reshape(1, BLK), theirs.reshape(1, BLK),
-        owner_map.reshape(1, -1), jnp.asarray(part_positions()), jnp.asarray(live_at),
+        samples, marks, counts.reshape(1, BLK), series.reshape(1, BLK), owner_map.reshape(1, -1),
+        jnp.asarray(part_positions()), jnp.asarray(live_at),
     )
 
 
@@ -597,9 +608,7 @@
 
 
 def body(samples, counts, buckets, block_series, owner_map):
-    swap = [(i, i ^ 1) for i in range(SHARDS)]
-    theirs = lax.ppermute(block_series, "shard", swap)
-    sk, ends, sums, meta, live = exchange_call(samples, buckets, counts, block_series, theirs, owner_map)
+    sk, ends, sums, meta, live = exchange_call(samples, buckets, counts, block_series, owner_map)
     cold, sketches, live_rows = finish_call(meta, ends, sums, sk, live)
     return cold.reshape(1, 1, SHARDS * CAP, 4, 8, LANES), sketches, live_rows
 

time: 68.5 us -> 59.8 us (0.87)
  Pallas kernels: 65.8 us -> 59.1 us
  waiting for transfers between devices: 1.28 us -> 0 us
    pallas_call x1, Pallas kernels: 62.6 us -> 55.9 us  [exchange_call(): pl.pallas_call(functools.partial(exchange_kernel, step=step), in_specs=[a...]
    ppermute x1 -> x0, waiting for transfers between devices: 1.28 us -> none  [body(): theirs = lax.ppermute(block_series, 'shard', swap)]
  transfers between devices with their start and end apart: 1 -> 0, of which waited for: 1 -> 0; matrix products, arithmetic and copies ran while one was open for 0% -> 0% of each run, Pallas kernels for 0% -> 0%
where the time goes in v6:
time: 59.8 us; the launch traced here: 59.7 us
  Pallas kernels  59.1 us (99%)
  between operations  0.64 us (1%)
    pallas_call x1, Pallas kernels, exchange_call(): pl.pallas_call(functools.partial(exchange_kernel, step=step), in_specs=[a...  55.9 us
    pallas_call x1, Pallas kernels, finish_call(): pl.pallas_call(functools.partial(finish_kernel, step=step), in_specs=[any...  3.19 us

profile of v6, /device:TPU:0, one launch (start us, length us, event | category | flops | bytes accessed | tf_op | source)
XLA Modules:
  0.0 59.7 jit_solution(1795753616196371337)
XLA Ops:
  0.6 55.9 %exchange.1 = (f32[2,128,128]{2,1,0:T(8,128)}, bf16[32,4,16,128]{3,2,1,0:T(8,128)(2,1)}, s32[32,4,4,128]{3,2,1,0:T(4,128)}, f32[32,1,128]{2,1,0:T(1,128)}, f32[1,128]{1,0:T(1,128)}) custom-call(bf16[64,480,128]{2,1,0:T(8,128)(2,1)} %samples.1, s32[64,480]{1,0:T(8,128)} %marks_ref.1, s32[1,64]{1,0:T(1,128)} %bitcast.5, s32[1,64]{1,0:T(1,128)} %bitcast.6, ...), custom_call_target="tpu_custom_call" | custom-call | tf_op jit(solution)/shard_map/exchange/pallas_call | solution.py:496
  56.5 3.2 %finish.1 = (f32[128,4,8,128]{3,2,1,0:T(8,128)}, f32[2,128,128]{2,1,0:T(8,128)}, f32[2]{0:T(128)}) custom-call(f32[32,1,128]{2,1,0:T(1,128)} %get-tuple-element.11.meta, bf16[32,4,16,128]{3,2,1,0:T(8,128)(2,1)} %get-tuple-element.12.ends, s32[32,4,4,128]{3,2,1,0:T(4,128)} %get-tuple-element.13.sums, f32[2,128,128]{2,1,0:T(8,128)} %get-tuple-element.14.sk_in, ...), custom_call_target="tpu_custom_call" | custom-call | tf_op jit(solution)/shard_map/finish/pallas_call | solution.py:586

commit v7 on v6

--- a/solution.py
+++ b/solution.py
@@ -20,6 +20,7 @@
 EVENTS = ((0, 0, 1), (0, 1, 1), (1, 0, 1), (1, 1, 1), (2, 0, 1), (4, 0, 1), (3, 1, 1), (2, 1, 1), (3, 0, 1), (6, 0, 1), (6, 1, 1), (4, 1, 1), (7, 1, 1), (5, 0, 1), (5, 1, 1), (0, 0, 2), (2, 1, 2), (3, 1, 2), (0, 1, 2), (7, 0, 1), (6, 0, 2), (3, 0, 2), (5, 0, 2), (1, 1, 2), (1, 0, 2), (4, 1, 2), (0, 0, 3), (2, 0, 2), (7, 1, 2), (4, 0, 2), (5, 1, 2), (6, 1, 2), (0, 1, 3), (3, 0, 3), (2, 1, 3), (7, 0, 2), (1, 1, 3), (3, 1, 3), (2, 0, 3), (6, 0, 3), (1, 0, 3), (4, 0, 3), (5, 0, 3), (5, 1, 3), (4, 1, 3), (6, 1, 3), (7, 1, 3), (7, 0, 3))
 TAILS = tuple(tuple(d for d in range(6) if d not in g[0]) for g in GROUPS)
 PARTS = len(GROUPS)
+READY = tuple(sorted(range(PARTS), key=lambda p: max(i for i, e in enumerate(EVENTS) if e[0] == p)))
 ROWS = BINS // PARTS
 LIMIT = 6.0
 LEVELS = 32766.0
@@ -346,12 +347,12 @@
         send(p, k * HALVINGS + s, spot(k, s), half, across((d,)))
         bases[p, k].append(bases[p, k][s] + bits[d] * half)
 
-    lax.fori_loop(0, 3, ends, 0)
+    lax.fori_loop(0, 2, ends, 0)
     series_copy.wait_recv()
     last_blocks(routing(their_series[...], map_row)[0], their_v, 0)
     their_copy = pltpu.make_async_copy(their_v, their_idx, idx_sem.at[1])
     their_copy.start()
-    lax.fori_loop(3, 7, ends, 0)
+    lax.fori_loop(2, 3, ends, 0)
     their_copy.wait()
     for p in parts:
         d2d(p).wait_recv()
@@ -363,7 +364,7 @@
             halve(p, k, 0)
             densify(p, k * 64 + bit * 32)
 
-    lax.fori_loop(7, BLK // 4, ends, 0)
+    lax.fori_loop(3, BLK // 4, ends, 0)
     lax.fori_loop(0, SHARDS, place, 0)
     for c in kept:
         c.start()
@@ -430,7 +431,7 @@
     for c in kept:
         c.wait()
 
-    for p in parts:
+    for p in READY:
         mine = bits[TAILS[p][0]] * 4 + bits[TAILS[p][1]] * 2 + bits[TAILS[p][2]]
         v = [acc[p][bases[p, k][HALVINGS] + mine] for k in range(2)]
         for m in range(1, 8):

time: 59.8 us -> 59.9 us (level)
  no operation moved by 1% of the time
where the time goes in v7:
time: 59.9 us; the launch traced here: 59.5 us
  Pallas kernels  58.8 us (98%)
  between operations  0.64 us (1%)
    pallas_call x1, Pallas kernels, exchange_call(): pl.pallas_call(functools.partial(exchange_kernel, step=step), in_specs=[a...  55.7 us
    pallas_call x1, Pallas kernels, finish_call(): pl.pallas_call(functools.partial(finish_kernel, step=step), in_specs=[any...  3.19 us

profile of v7, /device:TPU:0, one launch (start us, length us, event | category | flops | bytes accessed | tf_op | source)
XLA Modules:
  0.0 59.5 jit_solution(11042811948595132051)
XLA Ops:
  0.6 55.7 %exchange.1 = (f32[2,128,128]{2,1,0:T(8,128)}, bf16[32,4,16,128]{3,2,1,0:T(8,128)(2,1)}, s32[32,4,4,128]{3,2,1,0:T(4,128)}, f32[32,1,128]{2,1,0:T(1,128)}, f32[1,128]{1,0:T(1,128)}) custom-call(bf16[64,480,128]{2,1,0:T(8,128)(2,1)} %samples.1, s32[64,480]{1,0:T(8,128)} %marks_ref.1, s32[1,64]{1,0:T(1,128)} %bitcast.5, s32[1,64]{1,0:T(1,128)} %bitcast.6, ...), custom_call_target="tpu_custom_call" | custom-call | tf_op jit(solution)/shard_map/exchange/pallas_call | solution.py:497
  56.3 3.2 %finish.1 = (f32[128,4,8,128]{3,2,1,0:T(8,128)}, f32[2,128,128]{2,1,0:T(8,128)}, f32[2]{0:T(128)}) custom-call(f32[32,1,128]{2,1,0:T(1,128)} %get-tuple-element.11.meta, bf16[32,4,16,128]{3,2,1,0:T(8,128)(2,1)} %get-tuple-element.12.ends, s32[32,4,4,128]{3,2,1,0:T(4,128)} %get-tuple-element.13.sums, f32[2,128,128]{2,1,0:T(8,128)} %get-tuple-element.14.sk_in, ...), custom_call_target="tpu_custom_call" | custom-call | tf_op jit(solution)/shard_map/finish/pallas_call | solution.py:587
